TPU v7x, 256 devices: a whole 4x4x8 slice. The times are simulated.
256 devices in a mesh: grp: 4 (over y_lo, core), sp: 64 (over y_hi, z, x).
Axes of the slice: x: 4, y: 4 (y_hi: 2, y_lo: 2; y = y_hi * 2 + y_lo), z: 8, core: 2. Of those that a mesh axis runs over, the one named last changes fastest.
Arguments:
- flame_state: float32 [54, 128, 512], P(None, 'sp', 'grp'), may hold values from -1 to 2, as said below
- tangents: float32 [12, 54, 128, 512], P('grp', None, 'sp'), may hold values from -6 to 6
- direction_index: int32 [12], P('grp'), may hold values from 0 to 324
- reactant_table: int32 [325, 53], replicated, may hold values from 0 to 2, as said below
- product_table: int32 [325, 53], replicated, may hold values from 0 to 2, as said below
- natural_log_frequency: float32 [325], replicated, may hold values from -3 to -1
- arrhenius_energy: float32 [325], replicated, may hold values from 0.5 to 3
- diffusivity: float32 [54], replicated, may hold values from 0.03 to 0.25
- enthalpy: float32 [53], replicated, may hold values from -0.5 to 0.5
Outputs:
- new_state: float32 [54, 128, 512], P(None, 'sp', 'grp')
- new_tangents: float32 [12, 54, 128, 512], P('grp', None, 'sp')
Inputs may be any that keep to these rules, and one draw needn't show every extreme that they name: `flame_state`: rows 0 to 52 are log concentrations in [-1, 0.5]; the last row is temperature in [1, 2]. `reactant_table`: each reaction has one or two reactant units; a species may count twice. `product_table`: each reaction has one or two product units; a species may count twice.
All inputs are finite; a program needn't handle non-finite values.
Results may differ from a plain program's by a relative error of at most 0.0003.
Values sent between devices are 32-bit elements; how exact they have to be, the bound alone decides.
No kernel may reach another device: no remote copies, remote signals or barrier semaphores. Data moves between devices by JAX's collectives and lax.ppermute only.
A program may use at most 128 MiB of HBM per device.

v0:
```python
import jax
import jax.numpy as jnp
from jax import lax
from jax.experimental import pallas as pl
from jax.experimental.pallas import tpu as pltpu
from jax.sharding import Mesh
from jax.sharding import PartitionSpec as P

GRP = ("grp_0", "grp_1")
F = 54
FP = 56
RP = 336
TEMP = 53
f32 = jnp.float32
bf16 = jnp.bfloat16


def split(x):
    high = x.astype(bf16)
    return high, (x - high.astype(f32)).astype(bf16)


def rows_of(shape):
    return lax.broadcasted_iota(jnp.int32, shape, 0)


def exponents(x, weights, ones_from, ones_to):
    n = x.shape[1]
    high, low = split(jnp.concatenate([x, jnp.zeros((8, n), f32)], 0))
    row = rows_of((16, n))
    ones = jnp.where((row >= ones_from) & (row < ones_to), 1.0, 0.0)
    extra = jnp.where(row == 0, jnp.broadcast_to(x[TEMP : TEMP + 1, :], (16, n)), ones)
    rhs = jnp.concatenate([high, low, extra.astype(bf16)], 0)
    return jnp.dot(weights, rhs, preferred_element_type=f32)


def produced(rates, weights):
    high, low = split(rates)
    out = jnp.dot(weights, jnp.concatenate([high, low], 0), preferred_element_type=f32)
    last = out[48:56]
    heat = last + pltpu.roll(last, 7, 0) + pltpu.roll(last, 6, 0)
    row = rows_of(last.shape)
    last = jnp.where(row < 5, last, jnp.where(row == 5, heat, 0.0))
    return jnp.concatenate([out[:48], last], 0)


def with_last_row(x, value):
    last = jnp.where(rows_of((8, x.shape[1])) == 5, value, x[48:56])
    return jnp.concatenate([x[:48], last], 0)


def laplace(ref, p, j):
    c = ref[p, j]
    after = ref[p, (j + 1) & 3]
    before = ref[p, (j + 3) & 3]
    lane = lax.broadcasted_iota(jnp.int32, c.shape, 1)
    z = lane & 31
    total = pltpu.roll(jnp.where(lane >= 32, c, after), 96, 1)
    total = total + pltpu.roll(jnp.where(lane >= 96, before, c), 32, 1)
    total = total + jnp.where(z == 0, pltpu.roll(c, 97, 1), pltpu.roll(c, 1, 1))
    total = total + jnp.where(z == 31, pltpu.roll(c, 31, 1), pltpu.roll(c, 127, 1))
    return total + ref[p - 1, j] + ref[p + 1, j] - 6.0 * c


def near_kernel(place, own, even, odd, out):
    odd_side = place[0]
    pad = jnp.zeros((8, 512), f32)
    out[48:56, :] = pad
    sources = ((odd, 1 - odd_side), (own, odd_side), (own, 1 - odd_side), (even, odd_side))
    for p, (ref, start) in enumerate(sources):
        out[0:F, p * 128 : (p + 1) * 128] = ref[pl.ds(start, F, stride=2), :]


def nominal_section(x, w1, w2, rates_ref, aux_ref):
    n = x.shape[1]
    row = rows_of((8, n))
    temperature = jnp.broadcast_to(x[TEMP : TEMP + 1, :], (8, n))
    inverse_temperature = 1.0 / temperature
    rates = jnp.exp(exponents(with_last_row(x, -inverse_temperature), w1, 1, 4))
    rates_ref[...] = rates
    production = produced(rates, w2)
    inverse = jnp.exp(-x)
    last = jnp.where(row < 5, inverse[48:56], jnp.where(row == 5, 1.0, 0.0))
    inverse = jnp.concatenate([inverse[:48], last], 0)
    aux_ref[0:FP] = with_last_row(production, 0.0)
    aux_ref[FP : 2 * FP] = inverse
    aux_ref[2 * FP : 2 * FP + 8] = inverse_temperature * inverse_temperature
    return production * inverse


def nominal_kernel(place, own, core, other, other_core, even, odd, w1, w2, spread, rates_1, aux_1, rates_2, aux_2, out, state, slope, middle):
    odd_side = place[0]
    quarter = place[1]
    for blocks, k in ((own, 0), (core, 1), (other, 2), (other_core, 3)):
        for p in range(4):
            state[p + 1, quarter ^ k] = blocks[:, p * 128 : (p + 1) * 128]
    state[0, quarter, 48:56, :] = jnp.zeros((8, 128), f32)
    state[5, quarter, 48:56, :] = jnp.zeros((8, 128), f32)
    state[0, quarter, 0:F, :] = odd[pl.ds(odd_side, F, stride=2), :]
    state[5, quarter, 0:F, :] = even[pl.ds(1 - odd_side, F, stride=2), :]

    def first(step, carry):
        j = step >> 1
        half = step & 1
        p = 1 + 2 * half
        x = jnp.concatenate([state[p, j], state[p + 1, j]], 1)
        chem = nominal_section(x, w1[...], w2[...], rates_1.at[j, half], aux_1.at[j, half])
        slope[p, j] = chem[:, :128]
        slope[p + 1, j] = chem[:, 128:]
        return carry

    lax.fori_loop(0, 8, first, 0)

    def advance(p, j):
        s = slope[p, j] + spread[...] * laplace(state, p, j)
        slope[p, j] = s
        middle[p, j] = state[p, j] + 0.2 * s

    def diffuse(j, carry):
        advance(2, j)
        advance(3, j)
        return carry

    lax.fori_loop(0, 4, diffuse, 0)
    advance(1, quarter)
    advance(4, quarter)

    def second(j, carry):
        x = jnp.concatenate([middle[2, j], middle[3, j]], 1)
        chem = nominal_section(x, w1[...], w2[...], rates_2.at[j], aux_2.at[j])
        slope[2, j] = slope[2, j] + chem[:, :128]
        slope[3, j] = slope[3, j] + chem[:, 128:]
        return carry

    lax.fori_loop(0, 4, second, 0)
    for p, start in ((2, odd_side), (3, 1 - odd_side)):
        total = slope[p, quarter] + spread[...] * laplace(middle, p, quarter)
        new = state[p, quarter] + 0.1 * total
        out[pl.ds(start, F, stride=2), :] = new[0:F]


def tangent_section(u, w1, w2, rates, aux_ref):
    change_row = u[48:56] * aux_ref[2 * FP : 2 * FP + 8]
    change = exponents(with_last_row(u, change_row), w1, 4, 5)
    production_change = produced(rates * change, w2)
    return (production_change - aux_ref[0:FP] * u) * aux_ref[FP : 2 * FP]


def tangent_kernel(place, own, even, odd, rates_1, aux_1, rates_2, aux_2, w1, w2, spread, out, state, slope, middle):
    odd_side = place[0]
    sources = ((odd, odd_side), (odd, 1 - odd_side), (own, odd_side), (own, 1 - odd_side), (even, odd_side), (even, 1 - odd_side))
    for p, (ref, start) in enumerate(sources):
        for j in range(4):
            state[p, j, 48:56, :] = jnp.zeros((8, 128), f32)
            state[p, j, 0:F, :] = ref[pl.ds(start + 2 * j, F, stride=8), :]

    def first(step, carry):
        j = step >> 1
        half = step & 1
        p = 1 + 2 * half
        u = jnp.concatenate([state[p, j], state[p + 1, j]], 1)
        chem = tangent_section(u, w1[...], w2[...], rates_1[j, half], aux_1.at[j, half])
        slope[p, j] = chem[:, :128]
        slope[p + 1, j] = chem[:, 128:]
        return carry

    lax.fori_loop(0, 8, first, 0)

    def diffuse(j, carry):
        for p in range(1, 5):
            s = slope[p, j] + spread[...] * laplace(state, p, j)
            slope[p, j] = s
            middle[p, j] = state[p, j] + 0.2 * s
        return carry

    lax.fori_loop(0, 4, diffuse, 0)

    for j in range(4):
        u = jnp.concatenate([middle[2, j], middle[3, j]], 1)
        chem = tangent_section(u, w1[...], w2[...], rates_2[j], aux_2.at[j])
        for p, start in ((2, odd_side), (3, 1 - odd_side)):
            total = slope[p, j] + chem[:, (p - 2) * 128 : (p - 1) * 128] + spread[...] * laplace(middle, p, j)
            new = state[p, j] + 0.1 * total
            out[pl.ds(start + 2 * j, F, stride=8), :] = new[0:F]


def vmem(n):
    return [pl.BlockSpec(memory_space=pltpu.SMEM)] + [pl.BlockSpec(memory_space=pltpu.VMEM)] * n


def params():
    return pltpu.CompilerParams(vmem_limit_bytes=30 * 1024 * 1024)


def parts_of(x, count):
    parts = []
    for _ in range(count):
        part = lax.reduce_precision(x, 8, 7)
        parts.append(part)
        x = x - part
    return parts


def weights_of(reactant_table, product_table, log_frequency, energy, enthalpy, direction_index):
    reactions = reactant_table.shape[0]
    consumed = reactant_table.astype(f32)
    net = (product_table - reactant_table).astype(f32)
    high, low = parts_of(energy, 2)
    group = jnp.concatenate([consumed, high[:, None], jnp.zeros((reactions, 10), f32)], 1)
    extra = jnp.stack([low, *parts_of(log_frequency, 3)], 1)
    chosen = (jnp.arange(reactions, dtype=jnp.int32)[:, None] == direction_index[None, :]).astype(f32)
    first = []
    for d in range(direction_index.shape[0]):
        w = jnp.concatenate([group, group, extra, chosen[:, d : d + 1], jnp.zeros((reactions, 11), f32)], 1)
        first.append(jnp.pad(w, ((0, RP - reactions), (0, 0))).astype(bf16))
    heat = -jnp.sum(net * enthalpy[None, :], 1)
    rows = jnp.concatenate([net.T, jnp.stack(parts_of(heat, 3), 0), jnp.zeros((8, reactions), f32)], 0)
    rows = jnp.pad(rows, ((0, 0), (0, RP - reactions))).astype(bf16)
    return first, jnp.concatenate([rows, rows], 1)


def cell_rows(block):
    rows = block.reshape(*block.shape[:-1], 4, 128)
    return jnp.swapaxes(rows, -3, -2).reshape(-1, 128)


def shards(flame_state, tangents, direction_index, reactant_table, product_table, log_frequency, energy, diffusivity, enthalpy):
    count = lax.axis_size("sp")
    even = [(i, i ^ 1) for i in range(count)]
    odd = [(i, (i + 1 if i & 1 else i - 1) % count) for i in range(count)]
    swap = [(0, 1), (1, 0)]
    state_even = lax.ppermute(flame_state, "sp", even)
    state_odd = lax.ppermute(flame_state, "sp", odd)
    sides = []
    for d in range(3):
        sides.append((lax.ppermute(tangents[d], "sp", even), lax.ppermute(tangents[d], "sp", odd)))
    quarter = 2 * lax.axis_index("grp_0") + lax.axis_index("grp_1")
    place = jnp.stack([lax.axis_index("sp") & 1, quarter]).astype(jnp.int32)
    first, second = weights_of(reactant_table, product_table, log_frequency, energy, enthalpy, direction_index)
    spread = jnp.broadcast_to(jnp.pad(diffusivity, (0, FP - F))[:, None], (FP, 128))

    own_rows, even_rows, odd_rows = (x.reshape(2 * F, 128) for x in (flame_state, state_even, state_odd))
    near = pl.pallas_call(
        near_kernel,
        out_shape=jax.ShapeDtypeStruct((FP, 512), f32),
        in_specs=vmem(3),
        out_specs=pl.BlockSpec(memory_space=pltpu.VMEM),
        name="near_planes",
    )(place, own_rows, even_rows, odd_rows)
    other = lax.ppermute(near, "grp_0", swap)
    core = lax.ppermute(near, "grp_1", swap)
    other_core = lax.ppermute(other, "grp_1", swap)

    planes = pltpu.VMEM((6, 4, FP, 128), f32)
    aux_rows = 2 * FP + 8
    rates_1, aux_1, rates_2, aux_2, new_state = pl.pallas_call(
        nominal_kernel,
        out_shape=(
            jax.ShapeDtypeStruct((4, 2, RP, 256), f32),
            jax.ShapeDtypeStruct((4, 2, aux_rows, 256), f32),
            jax.ShapeDtypeStruct((4, RP, 256), f32),
            jax.ShapeDtypeStruct((4, aux_rows, 256), f32),
            jax.ShapeDtypeStruct((2 * F, 128), f32),
        ),
        in_specs=vmem(9),
        out_specs=tuple(pl.BlockSpec(memory_space=pltpu.VMEM) for _ in range(5)),
        scratch_shapes=[planes, planes, planes],
        compiler_params=params(),
        name="nominal",
    )(place, near, core, other, other_core, even_rows, odd_rows, first[0], second, spread)

    results = []
    for d in range(3):
        results.append(
            pl.pallas_call(
                tangent_kernel,
                out_shape=jax.ShapeDtypeStruct((8 * F, 128), f32),
                in_specs=vmem(10),
                out_specs=pl.BlockSpec(memory_space=pltpu.VMEM),
                scratch_shapes=[planes, planes, planes],
                compiler_params=params(),
                name="tangent",
            )(place, cell_rows(tangents[d]), cell_rows(sides[d][0]), cell_rows(sides[d][1]), rates_1, aux_1, rates_2, aux_2, first[d], second, spread)
        )
    rows = jnp.stack(results).reshape(3, F, 4, 2, 128)
    new_tangents = jnp.swapaxes(rows, 2, 3).reshape(tangents.shape)
    return new_state.reshape(flame_state.shape), new_tangents


def solution(mesh):
    split_mesh = Mesh(mesh.devices.reshape(2, 2, mesh.shape["sp"]), ("grp_0", "grp_1", "sp"))
    state = P(None, "sp", GRP)
    sensitivities = P(GRP, None, "sp", None)
    placed = (state, sensitivities, P(GRP), P(), P(), P(), P(), P(), P())
    return jax.shard_map(shards, mesh=split_mesh, in_specs=placed, out_specs=(state, sensitivities), check_vma=False)
```

profile of v0, /device:TPU:2, one launch (start us, length us, event | category | flops | bytes accessed | tf_op | source)
XLA Modules:
  0.0 86.8 jit_solution(18185403225218201886)
XLA Ops:
  0.7 2.3 %collective-permute-start = (f32[54,2,128]{2,1,0:T(2,128)}, f32[54,2,128]{2,1,0:T(2,128)S(1)}, u32[]{:S(2)}, u32[]{:S(2)}) collective-permute-start(f32[54,2,128]{2,1,0:T(2,128)} %param.9), channel_id=1, source_target_pairs={{0,1},{1,0},{2,3},{3,2},{4,5},{5,4},{6,7},{7,6},{8,9},{9,8},{10,11... | collective-permute-start | bytes 165896 | tf_op jit(solution)/shard_map/ppermute | solution.py:232
  3.5 2.4 %slice_bitcast_fusion.2 = (f32[54,2,512]{2,1,0:T(2,128)}, f32[54,2,512]{2,1,0:T(2,128)}, f32[54,2,512]{2,1,0:T(2,128)}, f32[1,54,2,512]{3,2,1,0:T(2,128)}, f32[1...) fusion(f32[3,54,2,512]{3,2,1,0:T(2,128)} %param.10), kind=kLoop, calls=%fused_computation.27 | loop fusion | bytes 1990656 | tf_op jit(solution)/shard_map/squeeze | solution.py:236
  5.9 1.6 %collective-permute-start.6 = (f32[54,2,512]{2,1,0:T(2,128)}, f32[54,2,512]{2,1,0:T(2,128)S(1)}, u32[]{:S(2)}, u32[]{:S(2)}) collective-permute-start(f32[54,2,512]{2,1,0:T(2,128)} %get-tuple-element.12), channel_id=1, source_target_pairs={{0,63},{1,2},{2,1},{3,4},{4,3},{5,6},{6,5},{7,8},{8,7},{9,10},{10,... | collective-permute-start | bytes 663560 | tf_op jit(solution)/shard_map/ppermute | solution.py:236
  7.5 7.8 %collective-permute-start.5 = (f32[54,2,512]{2,1,0:T(2,128)}, f32[54,2,512]{2,1,0:T(2,128)}, u32[]{:S(2)}, u32[]{:S(2)}) collective-permute-start(f32[54,2,512]{2,1,0:T(2,128)} %get-tuple-element.12), channel_id=1, source_target_pairs={{0,1},{1,0},{2,3},{3,2},{4,5},{5,4},{6,7},{7,6},{8,9},{9,8},{10,11... | collective-permute-start | bytes 663560 | tf_op jit(solution)/shard_map/ppermute | solution.py:236
  15.3 0.7 fusion.4
  16.8 1.0 %copy.22 = s32[325,53]{1,0:T(8,128)S(1)} copy(s32[325,53]{0,1:T(8,128)} %param.12) | data formatting | bytes 137800 | tf_op args[3]
  20.5 1.5 %near_planes.1.own = f32[56,512]{1,0:T(8,128)} custom-call(s32[2]{0:T(128)} %pad_add_fusion.place, f32[108,128]{1,0:T(8,128)} %reshape.105.own, f32[108,128]{1,0:T(8,128)} %reshape.106.even, f32[108,128]{1,0:T(8,128)} %reshape.107.odd), custom_call_target="tpu_custom_call" | custom-call | tf_op jit(solution)/shard_map/near_planes/pallas_call | solution.py:243
  23.4 2.5 %concatenate.24 = bf16[325,144]{1,0:T(8,128)(2,1)S(1)} concatenate(bf16[325,53]{1,0:T(8,128)(2,1)S(1)} %convert_convert_fusion.1, bf16[325,1]{1,0:T(8,128)(2,1)S(1)} %reshape.130, bf16[325,10]{1,0:T(8,128)(2,1)S(1)} %broadcast_in_dim.9, bf16[325,53]{1,0:T(8,128)(2,1)S(1)} %convert_convert_fusion.1, bf16[325,1]{1,0:T(8,128)(2,1)S(1)} %reshape.130, ...), dimensions={1} | concatenate | bytes 187200 | tf_op jit(solution)/shard_map/concatenate | solution.py:214
  26.0 1.1 %collective-permute-done.3.other = f32[56,512]{1,0:T(8,128)S(1)} collective-permute-done((f32[56,512]{1,0:T(8,128)}, f32[56,512]{1,0:T(8,128)S(1)}, u32[]{:S(2)}, u32[]{:S(2)}) %collective-permute-start.3) | collective-permute-done | bytes 114720 | tf_op jit(solution)/shard_map/ppermute | solution.py:250
  28.1 10.3 %collective-permute-start.9 = (f32[54,2,512]{2,1,0:T(2,128)}, f32[54,2,512]{2,1,0:T(2,128)}, u32[]{:S(2)}, u32[]{:S(2)}) collective-permute-start(f32[54,2,512]{2,1,0:T(2,128)} %get-tuple-element.14), channel_id=1, source_target_pairs={{0,1},{1,0},{2,3},{3,2},{4,5},{5,4},{6,7},{7,6},{8,9},{9,8},{10,11... | collective-permute-start | bytes 663560 | tf_op jit(solution)/shard_map/ppermute | solution.py:236
  39.2 2.5 %concatenate.27 = bf16[325,144]{1,0:T(8,128)(2,1)S(1)} concatenate(bf16[325,53]{1,0:T(8,128)(2,1)S(1)} %convert_convert_fusion.1, bf16[325,1]{1,0:T(8,128)(2,1)S(1)} %reshape.130, bf16[325,10]{1,0:T(8,128)(2,1)S(1)} %broadcast_in_dim.9, bf16[325,53]{1,0:T(8,128)(2,1)S(1)} %convert_convert_fusion.1, bf16[325,1]{1,0:T(8,128)(2,1)S(1)} %reshape.130, ...), dimensions={1} | concatenate | bytes 187200 | tf_op jit(solution)/shard_map/concatenate | solution.py:214
  41.6 0.7 pad.25.w1
  42.3 2.4 %concatenate.28 = bf16[325,144]{1,0:T(8,128)(2,1)S(1)} concatenate(bf16[325,53]{1,0:T(8,128)(2,1)S(1)} %convert_convert_fusion.1, bf16[325,1]{1,0:T(8,128)(2,1)S(1)} %reshape.130, bf16[325,10]{1,0:T(8,128)(2,1)S(1)} %broadcast_in_dim.9, bf16[325,53]{1,0:T(8,128)(2,1)S(1)} %convert_convert_fusion.1, bf16[325,1]{1,0:T(8,128)(2,1)S(1)} %reshape.130, ...), dimensions={1} | concatenate | bytes 187200 | tf_op jit(solution)/shard_map/concatenate | solution.py:214
  44.8 0.7 pad.26.w1
  45.7 0.8 copy-done.10
  46.5 0.8 copy-done.11
  47.3 0.9 %copy-done.12 = f32[56,512]{1,0:T(8,128)S(1)} copy-done((f32[56,512]{1,0:T(8,128)S(1)}, f32[56,512]{1,0:T(8,128)}, u32[]{:S(2)}) %copy-start.12) | copy-done | bytes 114712
  48.2 0.9 %copy-done.16 = f32[56,512]{1,0:T(8,128)S(1)} copy-done((f32[56,512]{1,0:T(8,128)S(1)}, f32[56,512]{1,0:T(8,128)}, u32[]{:S(2)}) %copy-start.16) | copy-done | bytes 114712
  49.1 0.9 %copy-done.18 = f32[56,512]{1,0:T(8,128)S(1)} copy-done((f32[56,512]{1,0:T(8,128)S(1)}, f32[56,512]{1,0:T(8,128)}, u32[]{:S(2)}) %copy-start.18) | copy-done | bytes 114712
  50.0 0.9 %copy-done.20 = f32[56,512]{1,0:T(8,128)S(1)} copy-done((f32[56,512]{1,0:T(8,128)S(1)}, f32[56,512]{1,0:T(8,128)}, u32[]{:S(2)}) %copy-start.20) | copy-done | bytes 114712
  50.9 6.7 %nominal.1 = (f32[4,2,336,256]{3,2,1,0:T(8,128)S(1)}, f32[4,2,120,256]{3,2,1,0:T(8,128)S(1)}, f32[4,336,256]{2,1,0:T(8,128)S(1)}, f32[4,120,256]{2,1,0:T(8,128)S(1)}, f32[108,128]{1,0:T(8,128)S(1)}) custom-call(s32[2]{0:T(128)S(1)} %copy-done.22, f32[56,512]{1,0:T(8,128)S(1)} %copy-done.12, f32[56,512]{1,0:T(8,128)S(1)} %copy-done.18, ...), custom_call_target="tpu_custom_call" | custom-call | tf_op jit(solution)/shard_map/nominal/pallas_call | solution.py:256
  57.7 1.1 %copy-done = f32[4,336,256]{2,1,0:T(8,128)} copy-done((f32[4,336,256]{2,1,0:T(8,128)}, f32[4,336,256]{2,1,0:T(8,128)S(1)}, u32[]{:S(2)}) %copy-start) | copy-done | bytes 1376280
  58.8 1.0 %copy-done.3 = f32[4,2,120,256]{3,2,1,0:T(8,128)} copy-done((f32[4,2,120,256]{3,2,1,0:T(8,128)}, f32[4,2,120,256]{3,2,1,0:T(8,128)S(1)}, u32[]{:S(2)}) %copy-start.3) | copy-done | bytes 983064
  60.4 1.5 %reshape.108 = f32[54,2,128]{2,1,0:T(2,128)} reshape(f32[108,128]{1,0:T(8,128)} %copy-done.21) | data formatting | bytes 110592 | tf_op jit(solution)/shard_map/reshape | solution.py:287
  61.8 1.3 %copy-done.1 = f32[4,336,256]{2,1,0:T(8,128)S(1)} copy-done((f32[4,336,256]{2,1,0:T(8,128)S(1)}, f32[4,336,256]{2,1,0:T(8,128)}, u32[]{:S(2)}) %copy-start.1) | copy-done | bytes 1376280
  63.2 1.2 %copy-done.4 = f32[4,2,120,256]{3,2,1,0:T(8,128)S(1)} copy-done((f32[4,2,120,256]{3,2,1,0:T(8,128)S(1)}, f32[4,2,120,256]{3,2,1,0:T(8,128)}, u32[]{:S(2)}) %copy-start.4) | copy-done | bytes 983064
  64.4 0.9 %copy-done.7 = f32[1,54,2,512]{3,2,1,0:T(2,128)S(1)} copy-done((f32[1,54,2,512]{3,2,1,0:T(2,128)S(1)}, f32[1,54,2,512]{3,2,1,0:T(2,128)}, u32[]{:S(2)}) %copy-start.7) | copy-done | bytes 221208
  65.3 0.9 %copy-done.14 = f32[54,2,512]{2,1,0:T(2,128)S(1)} copy-done((f32[54,2,512]{2,1,0:T(2,128)S(1)}, f32[54,2,512]{2,1,0:T(2,128)}, u32[]{:S(2)}) %copy-start.14) | copy-done | bytes 221208
  66.3 6.4 %tangent.3 = f32[432,128]{1,0:T(8,128)S(1)} custom-call(s32[2]{0:T(128)S(1)} %copy-done.22, f32[432,128]{1,0:T(8,128)S(1)} %bitcast.64, f32[432,128]{1,0:T(8,128)} %bitcast.9.even, f32[432,128]{1,0:T(8,128)S(1)} %bitcast.68, f32[4,2,336,256]{3,2,1,0:T(8,128)S(1)} %get-tuple-element.8.rates_1, f32[4,2,120,256]{3,2,1,0:T(8,128)S(1)} %copy-done.4, ...), custom_call_target="tpu_custom_call" | custom-call | tf_op jit(solution)/shard_map/tangent/pallas_call | solution.py:275
  72.7 6.5 %tangent.4 = f32[432,128]{1,0:T(8,128)S(1)} custom-call(s32[2]{0:T(128)S(1)} %copy-done.22, f32[432,128]{1,0:T(8,128)S(1)} %bitcast.63, f32[432,128]{1,0:T(8,128)} %bitcast.20.even, f32[432,128]{1,0:T(8,128)} %bitcast.23.odd, f32[4,2,336,256]{3,2,1,0:T(8,128)S(1)} %get-tuple-element.8.rates_1, f32[4,2,120,256]{3,2,1,0:T(8,128)S(1)} %copy-done.4, ...), custom_call_target="tpu_custom_call" | custom-call | tf_op jit(solution)/shard_map/tangent/pallas_call | solution.py:275
  79.2 6.4 %tangent.5 = f32[432,128]{1,0:T(8,128)S(1)} custom-call(s32[2]{0:T(128)S(1)} %copy-done.22, f32[432,128]{1,0:T(8,128)S(1)} %bitcast.62, f32[432,128]{1,0:T(8,128)} %bitcast.31.even, f32[432,128]{1,0:T(8,128)} %bitcast.34.odd, f32[4,2,336,256]{3,2,1,0:T(8,128)S(1)} %get-tuple-element.8.rates_1, f32[4,2,120,256]{3,2,1,0:T(8,128)S(1)} %copy-done.4, ...), custom_call_target="tpu_custom_call" | custom-call | tf_op jit(solution)/shard_map/tangent/pallas_call | solution.py:275
  85.7 1.1 %maximum_bitcast_fusion = f32[3,54,2,512]{3,2,1,0:T(2,128)} fusion(f32[1,54,4,2,128]{4,3,2,1,0:T(2,128)S(1)} %bitcast.67, f32[1,54,4,2,128]{4,3,2,1,0:T(2,128)S(1)} %bitcast.66, f32[1,54,4,2,128]{4,3,2,1,0:T(2,128)S(1)} %bitcast.65), kind=kLoop, calls=%fused_computation | loop fusion | flops 331776 | bytes 1327104 | tf_op jit(solution)/shard_map/reshape | solution.py:286
  (89 shorter events, 8.0 us)
Async XLA Ops:
  0.6 17.9 %copy-start.25 = (f32[54,2,128]{2,1,0:T(2,128)S(1)}, f32[54,2,128]{2,1,0:T(2,128)}, u32[]{:S(2)}) copy-start(f32[54,2,128]{2,1,0:T(2,128)} %param.9) | copy-start | bytes 165892
  0.6 17.2 %copy-start.23 = (s32[325,53]{0,1:T(8,128)S(1)}, s32[325,53]{0,1:T(8,128)}, u32[]{:S(2)}) copy-start(s32[325,53]{0,1:T(8,128)} %param.12) | copy-start | bytes 206704
  0.7 17.2 %copy-start.24 = (s32[325,53]{0,1:T(8,128)S(1)}, s32[325,53]{0,1:T(8,128)}, u32[]{:S(2)}) copy-start(s32[325,53]{0,1:T(8,128)} %param.13) | copy-start | bytes 206704
  0.7 22.1 %copy-start.26 = (f32[325]{0:T(512)S(1)}, f32[325]{0:T(512)}, u32[]{:S(2)}) copy-start(f32[325]{0:T(512)} %param.15) | copy-start | bytes 3904
  0.7 26.4 %copy-start.27 = (f32[53]{0:T(128)S(1)}, f32[53]{0:T(128)}, u32[]{:S(2)}) copy-start(f32[53]{0:T(128)} %param.17) | copy-start | bytes 640
  0.7 18.5 %collective-permute-start = (f32[54,2,128]{2,1,0:T(2,128)}, f32[54,2,128]{2,1,0:T(2,128)S(1)}, u32[]{:S(2)}, u32[]{:S(2)}) collective-permute-start(f32[54,2,128]{2,1,0:T(2,128)} %param.9), channel_id=1, source_target_pairs={{0,1},{1,0},{2,3},{3,2},{4,5},{5,4},{6,7},{7,6},{8,9},{9,8},{10,11... | collective-permute-start | bytes 165896 | tf_op jit(solution)/shard_map/ppermute | solution.py:232
  3.0 16.8 %collective-permute-start.1 = (f32[54,2,128]{2,1,0:T(2,128)}, f32[54,2,128]{2,1,0:T(2,128)S(1)}, u32[]{:S(2)}, u32[]{:S(2)}) collective-permute-start(f32[54,2,128]{2,1,0:T(2,128)} %param.9), channel_id=1, source_target_pairs={{0,63},{1,2},{2,1},{3,4},{4,3},{5,6},{6,5},{7,8},{8,7},{9,10},{10,... | collective-permute-start | bytes 165896 | tf_op jit(solution)/shard_map/ppermute | solution.py:233
  5.9 22.3 %collective-permute-start.6 = (f32[54,2,512]{2,1,0:T(2,128)}, f32[54,2,512]{2,1,0:T(2,128)S(1)}, u32[]{:S(2)}, u32[]{:S(2)}) collective-permute-start(f32[54,2,512]{2,1,0:T(2,128)} %get-tuple-element.12), channel_id=1, source_target_pairs={{0,63},{1,2},{2,1},{3,4},{4,3},{5,6},{6,5},{7,8},{8,7},{9,10},{10,... | collective-permute-start | bytes 663560 | tf_op jit(solution)/shard_map/ppermute | solution.py:236
  7.5 54.4 %collective-permute-start.5 = (f32[54,2,512]{2,1,0:T(2,128)}, f32[54,2,512]{2,1,0:T(2,128)}, u32[]{:S(2)}, u32[]{:S(2)}) collective-permute-start(f32[54,2,512]{2,1,0:T(2,128)} %get-tuple-element.12), channel_id=1, source_target_pairs={{0,1},{1,0},{2,3},{3,2},{4,5},{5,4},{6,7},{7,6},{8,9},{9,8},{10,11... | collective-permute-start | bytes 663560 | tf_op jit(solution)/shard_map/ppermute | solution.py:236
  15.2 57.4 %collective-permute-start.7 = (f32[54,2,512]{2,1,0:T(2,128)}, f32[54,2,512]{2,1,0:T(2,128)}, u32[]{:S(2)}, u32[]{:S(2)}) collective-permute-start(f32[54,2,512]{2,1,0:T(2,128)} %get-tuple-element.13), channel_id=1, source_target_pairs={{0,1},{1,0},{2,3},{3,2},{4,5},{5,4},{6,7},{7,6},{8,9},{9,8},{10,11... | collective-permute-start | bytes 663560 | tf_op jit(solution)/shard_map/ppermute | solution.py:236
  22.0 5.0 %collective-permute-start.3 = (f32[56,512]{1,0:T(8,128)}, f32[56,512]{1,0:T(8,128)S(1)}, u32[]{:S(2)}, u32[]{:S(2)}) collective-permute-start(f32[56,512]{1,0:T(8,128)} %near_planes.1.own), channel_id=1, source_target_pairs={{0,128},{128,0},{1,129},{129,1},{2,130},{130,2},{3,131},{131,3},{4... | collective-permute-start | bytes 344072 | tf_op jit(solution)/shard_map/ppermute | solution.py:250
  22.8 22.6 %copy-start.28 = (f32[54]{0:T(128)S(1)}, f32[54]{0:T(128)}, u32[]{:S(2)}) copy-start(f32[54]{0:T(128)} %param.16) | copy-start | bytes 652
  23.1 22.6 %copy-start.22 = (s32[2]{0:T(128)S(1)}, s32[2]{0:T(128)}, u32[]{:S(2)}) copy-start(s32[2]{0:T(128)} %pad_add_fusion.place) | copy-start | bytes 28
  25.9 1.6 %collective-permute-start.2 = (f32[56,512]{1,0:T(8,128)}, f32[56,512]{1,0:T(8,128)S(1)}, u32[]{:S(2)}, u32[]{:S(2)}) collective-permute-start(f32[56,512]{1,0:T(8,128)} %near_planes.1.own), channel_id=1, source_target_pairs={{0,64},{64,0},{1,65},{65,1},{2,66},{66,2},{3,67},{67,3},{4,68},{68... | collective-permute-start | bytes 344072 | tf_op jit(solution)/shard_map/ppermute | solution.py:251
  27.0 18.5 %copy-start.15 = (f32[56,512]{1,0:T(8,128)}, f32[56,512]{1,0:T(8,128)S(1)}, u32[]{:S(2)}) copy-start(f32[56,512]{1,0:T(8,128)S(1)} %collective-permute-done.3.other) | copy-start | bytes 344068
  27.0 11.4 %collective-permute-start.4 = (f32[56,512]{1,0:T(8,128)S(1)}, f32[56,512]{1,0:T(8,128)S(1)}, u32[]{:S(2)}, u32[]{:S(2)}) collective-permute-start(f32[56,512]{1,0:T(8,128)S(1)} %collective-permute-done.3.other), channel_id=1, source_target_pairs={{0,64},{64,0},{1,65},{65,1},{2,66},{66,2},{3,67},{67,3},{4,68},{68... | collective-permute-start | bytes 344072 | tf_op jit(solution)/shard_map/ppermute | solution.py:252
  28.1 44.5 %collective-permute-start.8 = (f32[54,2,512]{2,1,0:T(2,128)}, f32[54,2,512]{2,1,0:T(2,128)}, u32[]{:S(2)}, u32[]{:S(2)}) collective-permute-start(f32[54,2,512]{2,1,0:T(2,128)} %get-tuple-element.13), channel_id=1, source_target_pairs={{0,63},{1,2},{2,1},{3,4},{4,3},{5,6},{6,5},{7,8},{8,7},{9,10},{10,... | collective-permute-start | bytes 663560 | tf_op jit(solution)/shard_map/ppermute | solution.py:236
  28.1 17.3 %copy-start.13 = (f32[54,2,512]{2,1,0:T(2,128)}, f32[54,2,512]{2,1,0:T(2,128)S(1)}, u32[]{:S(2)}) copy-start(f32[54,2,512]{2,1,0:T(2,128)S(1)} %collective-permute-done.6) | copy-start | bytes 663556
  28.1 51.1 %collective-permute-start.9 = (f32[54,2,512]{2,1,0:T(2,128)}, f32[54,2,512]{2,1,0:T(2,128)}, u32[]{:S(2)}, u32[]{:S(2)}) collective-permute-start(f32[54,2,512]{2,1,0:T(2,128)} %get-tuple-element.14), channel_id=1, source_target_pairs={{0,1},{1,0},{2,3},{3,2},{4,5},{5,4},{6,7},{7,6},{8,9},{9,8},{10,11... | collective-permute-start | bytes 663560 | tf_op jit(solution)/shard_map/ppermute | solution.py:236
  39.1 40.2 %collective-permute-start.10 = (f32[54,2,512]{2,1,0:T(2,128)}, f32[54,2,512]{2,1,0:T(2,128)}, u32[]{:S(2)}, u32[]{:S(2)}) collective-permute-start(f32[54,2,512]{2,1,0:T(2,128)} %get-tuple-element.14), channel_id=1, source_target_pairs={{0,63},{1,2},{2,1},{3,4},{4,3},{5,6},{6,5},{7,8},{8,7},{9,10},{10,... | collective-permute-start | bytes 663560 | tf_op jit(solution)/shard_map/ppermute | solution.py:236
  47.3 0.9 %copy-start.12 = (f32[56,512]{1,0:T(8,128)S(1)}, f32[56,512]{1,0:T(8,128)}, u32[]{:S(2)}) copy-start(f32[56,512]{1,0:T(8,128)} %near_planes.1.own) | copy-start | bytes 344068
  57.6 1.1 %copy-start = (f32[4,336,256]{2,1,0:T(8,128)}, f32[4,336,256]{2,1,0:T(8,128)S(1)}, u32[]{:S(2)}) copy-start(f32[4,336,256]{2,1,0:T(8,128)S(1)} %get-tuple-element.10.rates_2) | copy-start | bytes 4128772
  58.8 1.0 %copy-start.3 = (f32[4,2,120,256]{3,2,1,0:T(8,128)}, f32[4,2,120,256]{3,2,1,0:T(8,128)S(1)}, u32[]{:S(2)}) copy-start(f32[4,2,120,256]{3,2,1,0:T(8,128)S(1)} %get-tuple-element.9.aux_1) | copy-start | bytes 2949124
  61.8 1.3 %copy-start.1 = (f32[4,336,256]{2,1,0:T(8,128)S(1)}, f32[4,336,256]{2,1,0:T(8,128)}, u32[]{:S(2)}) copy-start(f32[4,336,256]{2,1,0:T(8,128)} %copy-done) | copy-start | bytes 4128772
  63.2 1.2 %copy-start.4 = (f32[4,2,120,256]{3,2,1,0:T(8,128)S(1)}, f32[4,2,120,256]{3,2,1,0:T(8,128)}, u32[]{:S(2)}) copy-start(f32[4,2,120,256]{3,2,1,0:T(8,128)} %copy-done.3) | copy-start | bytes 2949124
  64.4 0.9 %copy-start.7 = (f32[1,54,2,512]{3,2,1,0:T(2,128)S(1)}, f32[1,54,2,512]{3,2,1,0:T(2,128)}, u32[]{:S(2)}) copy-start(f32[1,54,2,512]{3,2,1,0:T(2,128)} %get-tuple-element.15) | copy-start | bytes 663556
  65.3 0.9 %copy-start.14 = (f32[54,2,512]{2,1,0:T(2,128)S(1)}, f32[54,2,512]{2,1,0:T(2,128)}, u32[]{:S(2)}) copy-start(f32[54,2,512]{2,1,0:T(2,128)} %copy-done.13) | copy-start | bytes 663556
  66.3 6.4 %copy-start.2 = (f32[4,336,256]{2,1,0:T(8,128)S(1)}, f32[4,336,256]{2,1,0:T(8,128)}, u32[]{:S(2)}) copy-start(f32[4,336,256]{2,1,0:T(8,128)} %copy-done) | copy-start | bytes 4128772
  66.3 6.4 %copy-start.6 = (f32[1,54,2,512]{3,2,1,0:T(2,128)S(1)}, f32[1,54,2,512]{3,2,1,0:T(2,128)}, u32[]{:S(2)}) copy-start(f32[1,54,2,512]{3,2,1,0:T(2,128)} %get-tuple-element.17) | copy-start | bytes 663556
  66.3 6.4 %copy-start.9 = (bf16[336,144]{1,0:T(8,128)(2,1)S(1)}, bf16[336,144]{1,0:T(8,128)(2,1)}, u32[]{:S(2)}) copy-start(bf16[336,144]{1,0:T(8,128)(2,1)} %pad.25.w1) | copy-start | bytes 290308
  72.7 6.5 %copy-start.5 = (f32[1,54,2,512]{3,2,1,0:T(2,128)S(1)}, f32[1,54,2,512]{3,2,1,0:T(2,128)}, u32[]{:S(2)}) copy-start(f32[1,54,2,512]{3,2,1,0:T(2,128)} %get-tuple-element.16) | copy-start | bytes 663556
  72.7 6.5 %copy-start.8 = (bf16[336,144]{1,0:T(8,128)(2,1)S(1)}, bf16[336,144]{1,0:T(8,128)(2,1)}, u32[]{:S(2)}) copy-start(bf16[336,144]{1,0:T(8,128)(2,1)} %pad.26.w1) | copy-start | bytes 290308
  (8 other events, 6.2 us)
where the time goes:
time: 88 us; the launch traced here: 86.8 us
  local copies, waits for them, and re-layouts  30.2 us (34%)
  Pallas kernels  27.5 us (31%)
  starting transfers between devices  23.3 us (26%)
  other arithmetic  3.36 us (4%)
  waiting for transfers between devices  1.43 us (2%)
  between operations  1.04 us (1%)
    pallas_call x3, Pallas kernels, shards(): pl.pallas_call(tangent_kernel, out_shape=jax.ShapeDtypeStruct((8 * F, 128...  19.3 us
    ppermute x3, starting transfers between devices, shards(): lax.ppermute(tangents[d], 'sp', even)  18.2 us
    unnamed x59, local copies, waits for them, and re-layouts  14.7 us
    concatenate x3, local copies, waits for them, and re-layouts, weights_of(): jnp.concatenate([group, group, extra, chosen[:, d:d + 1], jnp.zeros((reac...  7.33 us
    pallas_call x1, Pallas kernels, shards(): pl.pallas_call(nominal_kernel, out_shape=(jax.ShapeDtypeStruct((4, 2, RP,...  6.75 us
    squeeze x1, local copies, waits for them, and re-layouts, shards(): tangents[d]  2.41 us
    ppermute x1, starting transfers between devices, shards(): state_even = lax.ppermute(flame_state, 'sp', even)  2.33 us
    reshape x3, local copies, waits for them, and re-layouts, shards(): x.reshape(2 * F, 128)  1.98 us
  transfers between devices with their start and end apart: 11, of which 2 were waited for; matrix products, arithmetic and copies ran while one was open for 22% of the time, Pallas kernels for 24%

commit v1 on v0

v1 whole, which is shorter than its diff:
```python
import functools

import jax
import jax.numpy as jnp
from jax import lax
from jax.experimental import pallas as pl
from jax.experimental.pallas import tpu as pltpu
from jax.sharding import Mesh
from jax.sharding import PartitionSpec as P

GRP = ("grp_0", "grp_1")
F = 54
FP = 56
RP = 336
TEMP = 53
f32 = jnp.float32
bf16 = jnp.bfloat16


def parts_of(x, count):
    parts = []
    for _ in range(count):
        part = x.astype(bf16).astype(f32)
        parts.append(part)
        x = x - part
    return parts


def rows_of(shape):
    return lax.broadcasted_iota(jnp.int32, shape, 0)


def exponents(x, weights, ones_from, ones_to):
    n = x.shape[1]
    row = rows_of((8, n))
    ones = jnp.where((row >= ones_from) & (row < ones_to), 1.0, 0.0)
    extra = jnp.where(row == 0, jnp.broadcast_to(x[TEMP : TEMP + 1, :], (8, n)), ones)
    high = jnp.concatenate([x, extra], 0).astype(bf16)
    low = (jnp.concatenate([x, extra], 0) - high.astype(f32)).astype(bf16)
    return jnp.dot(weights, jnp.concatenate([high, low], 0), preferred_element_type=f32)


def produced(rates, weights):
    high = rates.astype(bf16)
    low = (rates - high.astype(f32)).astype(bf16)
    out = jnp.dot(weights, high, preferred_element_type=f32) + jnp.dot(weights, low, preferred_element_type=f32)
    last = out[48:56]
    heat = last + pltpu.roll(last, 7, 0) + pltpu.roll(last, 6, 0)
    row = rows_of(last.shape)
    last = jnp.where(row < 5, last, jnp.where(row == 5, heat, 0.0))
    return jnp.concatenate([out[:48], last], 0)


def with_last_row(x, value):
    last = jnp.where(rows_of((8, x.shape[1])) == 5, value, x[48:56])
    return jnp.concatenate([x[:48], last], 0)


def laplace(ref, p, j):
    c = ref[p, j]
    after = ref[p, (j + 1) & 3]
    before = ref[p, (j + 3) & 3]
    lane = lax.broadcasted_iota(jnp.int32, c.shape, 1)
    z = lane & 31
    total = pltpu.roll(jnp.where(lane >= 32, c, after), 96, 1)
    total = total + pltpu.roll(jnp.where(lane >= 96, before, c), 32, 1)
    total = total + jnp.where(z == 0, pltpu.roll(c, 97, 1), pltpu.roll(c, 1, 1))
    total = total + jnp.where(z == 31, pltpu.roll(c, 31, 1), pltpu.roll(c, 127, 1))
    return total + ref[p - 1, j] + ref[p + 1, j] - 6.0 * c


def prepare_kernel(tangents, consumed, made, log_frequency, energy, diffusivity, enthalpy, chosen, t0, t1, t2, w1, w2, spread, sems):
    copies = [pltpu.make_async_copy(tangents.at[d], t, sems.at[d]) for d, t in enumerate((t0, t1, t2))]
    for copy in copies:
        copy.start()
    lanes = 384

    def wide(x):
        return jnp.pad(x, ((0, 0), (0, lanes - x.shape[1])))

    def row_of(ref):
        return wide(ref[...].reshape(1, ref.shape[0]))

    def placed(rows, shape):
        row = rows_of(shape)
        total = jnp.zeros(shape, f32)
        for k, value in rows.items():
            total = jnp.where(row == k, jnp.broadcast_to(value, shape), total)
        return total

    taken = wide(consumed[...].astype(f32))
    net = wide((made[...] - consumed[...]).astype(f32))
    high, low = parts_of(row_of(energy), 2)
    rows = {5: high, 8: low}
    for k, part in enumerate(parts_of(row_of(log_frequency), 3)):
        rows[9 + k] = part
    reaction = lax.broadcasted_iota(jnp.int32, (1, lanes), 1)
    for d in range(3):
        rows[12 + d] = (reaction == chosen[d]).astype(f32)
    zeros = jnp.zeros((11, lanes), f32)
    table = jnp.concatenate([taken, zeros], 0)
    table = jnp.concatenate([table[:48], table[48:64] + placed(rows, (16, lanes))], 0)
    w1[...] = jnp.concatenate([table, table], 0).T[:RP].astype(bf16)
    weighed = jnp.broadcast_to(jnp.pad(enthalpy[...].reshape(1, F - 1), ((0, 0), (0, 11))), (8, 64))
    table = jnp.concatenate([net, zeros], 0)
    heat = -jnp.dot(weighed, table, precision=lax.Precision.HIGHEST, preferred_element_type=f32)[:1]
    rows = {5 + k: part for k, part in enumerate(parts_of(heat, 3))}
    table = jnp.concatenate([table[:48], table[48:64] + placed(rows, (16, lanes))], 0)
    w2[...] = table[:, :RP].astype(bf16)
    spread[...] = jnp.broadcast_to(jnp.pad(diffusivity[...].reshape(1, F), ((0, 0), (0, 128 - F))), (128, 128)).T[:FP]
    for copy in copies:
        copy.wait()


def sides_of():
    return lax.axis_index("sp") & 1


def near_kernel(own, even, odd, out):
    odd_side = sides_of()
    out[48:56, :] = jnp.zeros((8, 512), f32)
    sources = ((odd, 1 - odd_side), (own, odd_side), (own, 1 - odd_side), (even, odd_side))
    for p, (ref, plane) in enumerate(sources):
        out[0:F, p * 128 : (p + 1) * 128] = ref[:, plane, :]


def nominal_section(x, w1, w2, rates_ref, aux_ref):
    n = x.shape[1]
    row = rows_of((8, n))
    temperature = jnp.broadcast_to(x[TEMP : TEMP + 1, :], (8, n))
    inverse_temperature = 1.0 / temperature
    rates = jnp.exp(exponents(with_last_row(x, -inverse_temperature), w1, 1, 4))
    rates_ref[...] = rates
    production = produced(rates, w2)
    inverse = jnp.exp(-x)
    last = jnp.where(row < 5, inverse[48:56], jnp.where(row == 5, 1.0, 0.0))
    inverse = jnp.concatenate([inverse[:48], last], 0)
    aux_ref[0:FP] = with_last_row(production, 0.0)
    aux_ref[FP : 2 * FP] = inverse
    aux_ref[2 * FP : 2 * FP + 8] = inverse_temperature * inverse_temperature
    return production * inverse


def planes_at(ref, first, last, j):
    return jnp.concatenate([ref[p, j] for p in range(first, last + 1)], 1)


def nominal_kernel(own, core, other, other_core, even, odd, w1, w2, spread, rates_1, aux_1, rates_2, aux_2, out, state, slope, middle):
    odd_side = sides_of()
    quarter = 2 * lax.axis_index("grp_0") + lax.axis_index("grp_1")
    for blocks, k in ((own, 0), (core, 1), (other, 2), (other_core, 3)):
        for p in range(4):
            state[p + 1, quarter ^ k] = blocks[:, p * 128 : (p + 1) * 128]
    state[0, quarter, 48:56, :] = jnp.zeros((8, 128), f32)
    state[5, quarter, 48:56, :] = jnp.zeros((8, 128), f32)
    state[0, quarter, 0:F, :] = odd[:, odd_side, :]
    state[5, quarter, 0:F, :] = even[:, 1 - odd_side, :]

    def first(j, carry):
        chem = nominal_section(planes_at(state, 1, 4, j), w1[...], w2[...], rates_1.at[j], aux_1.at[j])
        for p in range(4):
            slope[p + 1, j] = chem[:, p * 128 : (p + 1) * 128]
        return carry

    lax.fori_loop(0, 4, first, 0)

    def advance(p, j):
        s = slope[p, j] + spread[...] * laplace(state, p, j)
        slope[p, j] = s
        middle[p, j] = state[p, j] + 0.2 * s

    def diffuse(j, carry):
        advance(2, j)
        advance(3, j)
        return carry

    lax.fori_loop(0, 4, diffuse, 0)
    advance(1, quarter)
    advance(4, quarter)

    def second(j, carry):
        chem = nominal_section(planes_at(middle, 2, 3, j), w1[...], w2[...], rates_2.at[j], aux_2.at[j])
        slope[2, j] = slope[2, j] + chem[:, :128]
        slope[3, j] = slope[3, j] + chem[:, 128:]
        return carry

    lax.fori_loop(0, 4, second, 0)
    for p, plane in ((2, odd_side), (3, 1 - odd_side)):
        total = slope[p, quarter] + spread[...] * laplace(middle, p, quarter)
        new = state[p, quarter] + 0.1 * total
        out[:, plane, :] = new[0:F]


def tangent_section(u, w1, w2, rates_ref, aux_ref, d):
    change_row = u[48:56] * aux_ref[2 * FP : 2 * FP + 8]
    change = exponents(with_last_row(u, change_row), w1, 4 + d, 5 + d)
    production_change = produced(rates_ref[...] * change, w2)
    return (production_change - aux_ref[0:FP] * u) * aux_ref[FP : 2 * FP]


def tangent_kernel(own, even, odd, rates_1, aux_1, rates_2, aux_2, w1, w2, spread, *rest, d):
    out, result, state, slope, middle, sem = rest[-6:]
    odd_side = sides_of()
    sources = ((odd, odd_side), (odd, 1 - odd_side), (own, odd_side), (own, 1 - odd_side), (even, odd_side), (even, 1 - odd_side))
    for p, (ref, start) in enumerate(sources):
        for j in range(4):
            state[p, j, 48:56, :] = jnp.zeros((8, 128), f32)
            state[p, j, 0:F, :] = ref[pl.ds(start + 2 * j, F, stride=8), :]

    def first(j, carry):
        chem = tangent_section(planes_at(state, 1, 4, j), w1[...], w2[...], rates_1.at[j], aux_1.at[j], d)
        for p in range(4):
            slope[p + 1, j] = chem[:, p * 128 : (p + 1) * 128]
        return carry

    lax.fori_loop(0, 4, first, 0)

    def diffuse(j, carry):
        for p in range(1, 5):
            s = slope[p, j] + spread[...] * laplace(state, p, j)
            slope[p, j] = s
            middle[p, j] = state[p, j] + 0.2 * s
        return carry

    lax.fori_loop(0, 4, diffuse, 0)

    def second(j, carry):
        chem = tangent_section(planes_at(middle, 2, 3, j), w1[...], w2[...], rates_2.at[j], aux_2.at[j], d)
        for p, start in ((2, odd_side), (3, 1 - odd_side)):
            total = slope[p, j] + chem[:, (p - 2) * 128 : (p - 1) * 128] + spread[...] * laplace(middle, p, j)
            new = state[p, j] + 0.1 * total
            result[pl.ds(start + 2 * j, F, stride=8), :] = new[0:F]
        return carry

    lax.fori_loop(0, 4, second, 0)
    copy = pltpu.make_async_copy(result, out.at[pl.ds(d * 8 * F, 8 * F)], sem)
    copy.start()
    copy.wait()


VMEM = pl.BlockSpec(memory_space=pltpu.VMEM)
HBM = pl.BlockSpec(memory_space=pl.ANY)


def params(mebibytes):
    return pltpu.CompilerParams(vmem_limit_bytes=mebibytes * 1024 * 1024)


def cell_rows(block):
    rows = block.reshape(*block.shape[:-1], 4, 128)
    return jnp.swapaxes(rows, -3, -2).reshape(-1, 128)


def shards(flame_state, tangents, direction_index, reactant_table, product_table, log_frequency, energy, diffusivity, enthalpy):
    count = lax.axis_size("sp")
    even = [(i, i ^ 1) for i in range(count)]
    odd = [(i, (i + 1 if i & 1 else i - 1) % count) for i in range(count)]
    swap = [(0, 1), (1, 0)]
    state_even = lax.ppermute(flame_state, "sp", even)
    state_odd = lax.ppermute(flame_state, "sp", odd)
    *slices, w1, w2, spread = pl.pallas_call(
        prepare_kernel,
        out_shape=(
            *[jax.ShapeDtypeStruct(tangents.shape[1:], f32)] * 3,
            jax.ShapeDtypeStruct((RP, 128), bf16),
            jax.ShapeDtypeStruct((64, RP), bf16),
            jax.ShapeDtypeStruct((FP, 128), f32),
        ),
        in_specs=[HBM, *[VMEM] * 6, pl.BlockSpec(memory_space=pltpu.SMEM)],
        out_specs=(HBM, HBM, HBM, VMEM, VMEM, VMEM),
        scratch_shapes=[pltpu.SemaphoreType.DMA((3,))],
        compiler_params=params(4),
        name="prepare",
    )(tangents, reactant_table.T, product_table.T, log_frequency, energy, diffusivity, enthalpy, direction_index)
    sides = [(lax.ppermute(t, "sp", even), lax.ppermute(t, "sp", odd)) for t in slices]

    near = pl.pallas_call(
        near_kernel,
        out_shape=jax.ShapeDtypeStruct((FP, 512), f32),
        in_specs=[VMEM] * 3,
        out_specs=VMEM,
        compiler_params=params(2),
        name="near_planes",
    )(flame_state, state_even, state_odd)
    other = lax.ppermute(near, "grp_0", swap)
    core = lax.ppermute(near, "grp_1", swap)
    other_core = lax.ppermute(other, "grp_1", swap)

    planes = pltpu.VMEM((6, 4, FP, 128), f32)
    aux_rows = 2 * FP + 8
    rates_1, aux_1, rates_2, aux_2, new_state = pl.pallas_call(
        nominal_kernel,
        out_shape=(
            jax.ShapeDtypeStruct((4, RP, 512), f32),
            jax.ShapeDtypeStruct((4, aux_rows, 512), f32),
            jax.ShapeDtypeStruct((4, RP, 256), f32),
            jax.ShapeDtypeStruct((4, aux_rows, 256), f32),
            jax.ShapeDtypeStruct(flame_state.shape, f32),
        ),
        in_specs=[VMEM] * 9,
        out_specs=(VMEM,) * 5,
        scratch_shapes=[planes, planes, planes],
        compiler_params=params(10),
        name="nominal",
    )(near, core, other, other_core, state_even, state_odd, w1, w2, spread)

    rows = None
    for d in range(3):
        operands = [cell_rows(slices[d]), cell_rows(sides[d][0]), cell_rows(sides[d][1]), rates_1, aux_1, rates_2, aux_2, w1, w2, spread]
        if d:
            operands.append(rows)
        rows = pl.pallas_call(
            functools.partial(tangent_kernel, d=d),
            out_shape=jax.ShapeDtypeStruct((3 * 8 * F, 128), f32),
            in_specs=[VMEM] * 10 + [HBM] * (d > 0),
            out_specs=HBM,
            scratch_shapes=[pltpu.VMEM((8 * F, 128), f32), planes, planes, planes, pltpu.SemaphoreType.DMA],
            input_output_aliases={10: 0} if d else {},
            compiler_params=params(10),
            name="tangent",
        )(*operands)
    rows = rows.reshape(3, F, 4, 2, 128)
    return new_state, jnp.swapaxes(rows, 2, 3).reshape(tangents.shape)


def solution(mesh):
    split_mesh = Mesh(mesh.devices.reshape(2, 2, mesh.shape["sp"]), ("grp_0", "grp_1", "sp"))
    state = P(None, "sp", GRP)
    sensitivities = P(GRP, None, "sp", None)
    placed = (state, sensitivities, P(GRP), P(), P(), P(), P(), P(), P())
    return jax.shard_map(shards, mesh=split_mesh, in_specs=placed, out_specs=(state, sensitivities), check_vma=False)
```

time: 88 us -> 63.8 us (0.72); the launches traced: 86.8 us -> 63.5 us
  local copies, waits for them, and re-layouts: 30.2 us -> 7.01 us
  starting transfers between devices: 23.3 us -> 28.1 us
  Pallas kernels: 27.5 us -> 23.7 us
  other arithmetic: 3.36 us -> 0 us
  waiting for transfers between devices: 1.43 us -> 3.94 us
    unnamed x59 -> x18, local copies, waits for them, and re-layouts: 14.7 us -> 7.01 us
    concatenate x4 -> x0, local copies, waits for them, and re-layouts: 7.39 us -> none  [the longest x3 7.33 us: weights_of(): jnp.concatenate([group, group, extra, chosen[:, d:d + 1], jnp.zeros((reac...]
    ppermute x6, starting transfers between devices: 19.7 us -> 24.7 us  [the longest x3 22.7 us: shards(): lax.ppermute(t, 'sp', even)]
    reshape x4 -> x0, local copies, waits for them, and re-layouts: 3.45 us -> none  [the longest x3 1.98 us: shards(): x.reshape(2 * F, 128)]
    squeeze x1 -> x0, local copies, waits for them, and re-layouts: 2.41 us -> none  [shards(): tangents[d]]
    pallas_call x4 -> x5, Pallas kernels: 26 us -> 23.7 us  [the longest x3 16.5 us: shards(): pl.pallas_call(functools.partial(tangent_kernel, d=d), out_shape=jax.Shap...]
    ppermute x1, waiting for transfers between devices: 0.01 us -> 2.02 us  [shards(): state_odd = lax.ppermute(flame_state, 'sp', odd)]
    another operation x6 -> x0, other arithmetic: 2.01 us -> none
  transfers between devices with their start and end apart: 11 -> 11, of which waited for: 2 -> 2; matrix products, arithmetic and copies ran while one was open for 22% -> 0% of each run, Pallas kernels for 24% -> 29%
where the time goes in v1:
time: 63.8 us; the launch traced here: 63.5 us
  starting transfers between devices  28.1 us (44%)
  Pallas kernels  23.7 us (37%)
  local copies, waits for them, and re-layouts  7.01 us (11%)
  waiting for transfers between devices  3.94 us (6%)
  between operations  0.71 us (1%)
    ppermute x3, starting transfers between devices, shards(): lax.ppermute(t, 'sp', even)  22.7 us
    pallas_call x3, Pallas kernels, shards(): pl.pallas_call(functools.partial(tangent_kernel, d=d), out_shape=jax.Shap...  16.5 us
    unnamed x18, local copies, waits for them, and re-layouts  7.01 us
    pallas_call x1, Pallas kernels, shards(): pl.pallas_call(nominal_kernel, out_shape=(jax.ShapeDtypeStruct((4, RP, 51...  5.51 us
    ppermute x1, starting transfers between devices, shards(): state_even = lax.ppermute(flame_state, 'sp', even)  2.33 us
    ppermute x3, starting transfers between devices, shards(): lax.ppermute(t, 'sp', odd)  2.03 us
    ppermute x1, waiting for transfers between devices, shards(): state_odd = lax.ppermute(flame_state, 'sp', odd)  2.02 us
    ppermute x1, waiting for transfers between devices, shards(): state_even = lax.ppermute(flame_state, 'sp', even)  1.9 us
  transfers between devices with their start and end apart: 11, of which 2 were waited for; matrix products, arithmetic and copies ran while one was open for 0% of the time, Pallas kernels for 29%

profile of v1, /device:TPU:2, one launch (start us, length us, event | category | flops | bytes accessed | tf_op | source)
XLA Modules:
  0.0 63.5 jit_solution(10455125928357453943)
XLA Ops:
  0.6 2.3 %collective-permute-start = (f32[54,2,128]{2,1,0:T(2,128)}, f32[54,2,128]{2,1,0:T(2,128)S(1)}, u32[]{:S(2)}, u32[]{:S(2)}) collective-permute-start(f32[54,2,128]{2,1,0:T(2,128)} %own.1), channel_id=1, source_target_pairs={{0,1},{1,0},{2,3},{3,2},{4,5},{5,4},{6,7},{7,6},{8,9},{9,8},{10,11... | collective-permute-start | bytes 165896 | tf_op jit(solution)/shard_map/ppermute | solution.py:259
  3.0 0.4 collective-permute-start.1
  3.4 1.9 %collective-permute-done.even = f32[54,2,128]{2,1,0:T(2,128)S(1)} collective-permute-done((f32[54,2,128]{2,1,0:T(2,128)}, f32[54,2,128]{2,1,0:T(2,128)S(1)}, u32[]{:S(2)}, u32[]{:S(2)}) %collective-permute-start) | collective-permute-done | bytes 55328 | tf_op jit(solution)/shard_map/ppermute | solution.py:259
  5.3 2.0 %collective-permute-done.1.odd = f32[54,2,128]{2,1,0:T(2,128)S(1)} collective-permute-done((f32[54,2,128]{2,1,0:T(2,128)}, f32[54,2,128]{2,1,0:T(2,128)S(1)}, u32[]{:S(2)}, u32[]{:S(2)}) %collective-permute-start.1) | collective-permute-done | bytes 55328 | tf_op jit(solution)/shard_map/ppermute | solution.py:260
  7.3 0.8 %copy-done.3 = f32[54,2,128]{2,1,0:T(2,128)S(1)} copy-done((f32[54,2,128]{2,1,0:T(2,128)S(1)}, f32[54,2,128]{2,1,0:T(2,128)}, u32[]{:S(2)}) %copy-start.3) | copy-done | bytes 55320
  8.1 0.1 near_planes.1.own
  8.2 0.1 collective-permute-start.3
  8.3 1.1 %copy-done = f32[3,54,2,512]{3,2,1,0:T(2,128)S(1)} copy-done((f32[3,54,2,512]{3,2,1,0:T(2,128)S(1)}, f32[3,54,2,512]{3,2,1,0:T(2,128)}, u32[]{:S(2)}) %copy-start) | copy-done | bytes 663576
  9.4 0.9 %copy-done.1 = s32[325,53]{0,1:T(8,128)S(1)} copy-done((s32[325,53]{0,1:T(8,128)S(1)}, s32[325,53]{0,1:T(8,128)}, u32[]{:S(2)}) %copy-start.1) | copy-done | bytes 68924
  10.3 0.9 %copy-done.2 = s32[325,53]{0,1:T(8,128)S(1)} copy-done((s32[325,53]{0,1:T(8,128)S(1)}, s32[325,53]{0,1:T(8,128)}, u32[]{:S(2)}) %copy-start.2) | copy-done | bytes 68924
  11.2 0.7 %copy-done.4 = f32[325]{0:T(512)S(1)} copy-done((f32[325]{0:T(512)S(1)}, f32[325]{0:T(512)}, u32[]{:S(2)}) %copy-start.4) | copy-done | bytes 1324
  11.9 0.7 %copy-done.5 = f32[325]{0:T(512)S(1)} copy-done((f32[325]{0:T(512)S(1)}, f32[325]{0:T(512)}, u32[]{:S(2)}) %copy-start.5) | copy-done | bytes 1324
  12.6 0.7 %copy-done.6 = f32[54]{0:T(128)S(1)} copy-done((f32[54]{0:T(128)S(1)}, f32[54]{0:T(128)}, u32[]{:S(2)}) %copy-start.6) | copy-done | bytes 240
  13.2 0.7 %copy-done.7 = f32[53]{0:T(128)S(1)} copy-done((f32[53]{0:T(128)S(1)}, f32[53]{0:T(128)}, u32[]{:S(2)}) %copy-start.7) | copy-done | bytes 236
  13.9 0.7 %copy-done.8 = s32[3]{0:T(128)S(1)} copy-done((s32[3]{0:T(128)S(1)}, s32[3]{0:T(128)}, u32[]{:S(2)}) %copy-start.8) | copy-done | bytes 36
  14.5 1.6 %prepare.1 = (f32[54,2,512]{2,1,0:T(2,128)S(1)}, f32[54,2,512]{2,1,0:T(2,128)S(1)}, f32[54,2,512]{2,1,0:T(2,128)S(1)}, bf16[336,128]{1,0:T(8,128)(2,1)S(1)}, bf1...) custom-call(f32[3,54,2,512]{3,2,1,0:T(2,128)S(1)} %copy-done, s32[53,325]{1,0:T(8,128)S(1)} %bitcast.61, ...), custom_call_target="tpu_custom_call" | custom-call | tf_op jit(solution)/shard_map/prepare/pallas_call | solution.py:261
  16.2 8.5 %collective-permute-start.9 = (f32[54,2,512]{2,1,0:T(2,128)S(1)}, f32[54,2,512]{2,1,0:T(2,128)S(1)}, u32[]{:S(2)}, u32[]{:S(2)}) collective-permute-start(f32[54,2,512]{2,1,0:T(2,128)S(1)} %get-tuple-element.23), channel_id=1, source_target_pairs={{0,1},{1,0},{2,3},{3,2},{4,5},{5,4},{6,7},{7,6},{8,9},{9,8},{10,11... | collective-permute-start | bytes 663560 | tf_op jit(solution)/shard_map/ppermute | solution.py:275
  24.7 0.0 collective-permute-start.2
  24.7 0.0 collective-permute-done.3.other
  24.7 0.5 collective-permute-start.4
  25.2 8.4 %collective-permute-start.7 = (f32[54,2,512]{2,1,0:T(2,128)S(1)}, f32[54,2,512]{2,1,0:T(2,128)S(1)}, u32[]{:S(2)}, u32[]{:S(2)}) collective-permute-start(f32[54,2,512]{2,1,0:T(2,128)S(1)} %get-tuple-element.22), channel_id=1, source_target_pairs={{0,1},{1,0},{2,3},{3,2},{4,5},{5,4},{6,7},{7,6},{8,9},{9,8},{10,11... | collective-permute-start | bytes 663560 | tf_op jit(solution)/shard_map/ppermute | solution.py:275
  33.6 0.0 collective-permute-done.9
  33.6 2.0 %collective-permute-start.6 = (f32[54,2,512]{2,1,0:T(2,128)S(1)}, f32[54,2,512]{2,1,0:T(2,128)S(1)}, u32[]{:S(2)}, u32[]{:S(2)}) collective-permute-start(f32[54,2,512]{2,1,0:T(2,128)S(1)} %get-tuple-element.17), channel_id=1, source_target_pairs={{0,63},{1,2},{2,1},{3,4},{4,3},{5,6},{6,5},{7,8},{8,7},{9,10},{10,... | collective-permute-start | bytes 663560 | tf_op jit(solution)/shard_map/ppermute | solution.py:275
  35.7 0.0 collective-permute-done.4.other_core
  35.7 5.7 %collective-permute-start.5 = (f32[54,2,512]{2,1,0:T(2,128)S(1)}, f32[54,2,512]{2,1,0:T(2,128)S(1)}, u32[]{:S(2)}, u32[]{:S(2)}) collective-permute-start(f32[54,2,512]{2,1,0:T(2,128)S(1)} %get-tuple-element.17), channel_id=1, source_target_pairs={{0,1},{1,0},{2,3},{3,2},{4,5},{5,4},{6,7},{7,6},{8,9},{9,8},{10,11... | collective-permute-start | bytes 663560 | tf_op jit(solution)/shard_map/ppermute | solution.py:275
  41.4 5.5 %nominal.1 = (f32[4,336,512]{2,1,0:T(8,128)S(1)}, f32[4,120,512]{2,1,0:T(8,128)S(1)}, f32[4,336,256]{2,1,0:T(8,128)S(1)}, f32[4,120,256]{2,1,0:T(8,128)S(1)}, f32[54,2,128]{2,1,0:T(2,128)}) custom-call(f32[56,512]{1,0:T(8,128)S(1)} %near_planes.1.own, f32[56,512]{1,0:T(8,128)S(1)} %collective-permute-done.2.core, ...), custom_call_target="tpu_custom_call" | custom-call | tf_op jit(solution)/shard_map/nominal/pallas_call | solution.py:291
  46.9 5.5 %tangent.3.rest_0_ = f32[1296,128]{1,0:T(8,128)} custom-call(f32[432,128]{1,0:T(8,128)S(1)} %bitcast.52, f32[432,128]{1,0:T(8,128)S(1)} %bitcast.53, f32[432,128]{1,0:T(8,128)S(1)} %bitcast.54, f32[4,336,512]{2,1,0:T(8,128)S(1)} %get-tuple-element.18.rates_1, f32[4,120,512]{2,1,0:T(8,128)S(1)} %get-tuple-element.19.aux_1, ...), custom_call_target="tpu_custom_call" | custom-call | tf_op jit(solution)/shard_map/tangent/pallas_call | solution.py:312
  52.4 0.0 collective-permute-done.7
  52.4 0.0 collective-permute-done.8
  52.4 5.5 %tangent.4.rest_0_ = f32[1296,128]{1,0:T(8,128)} custom-call(f32[432,128]{1,0:T(8,128)S(1)} %bitcast.56, f32[432,128]{1,0:T(8,128)S(1)} %bitcast.57, f32[432,128]{1,0:T(8,128)S(1)} %bitcast.59, f32[4,336,512]{2,1,0:T(8,128)S(1)} %get-tuple-element.18.rates_1, f32[4,120,512]{2,1,0:T(8,128)S(1)} %get-tuple-element.19.aux_1, ...), custom_call_target="tpu_custom_call", output_to_operand_aliasing={{}: (10, {})} | custom-call | tf_op jit(solution)/shard_map/tangent/pallas_call | solution.py:312
  58.0 0.0 collective-permute-done.5
  58.0 5.5 %tangent.5 = f32[1296,128]{1,0:T(8,128)} custom-call(f32[432,128]{1,0:T(8,128)S(1)} %bitcast.55, f32[432,128]{1,0:T(8,128)S(1)} %bitcast.60, f32[432,128]{1,0:T(8,128)S(1)} %bitcast.58, f32[4,336,512]{2,1,0:T(8,128)S(1)} %get-tuple-element.18.rates_1, f32[4,120,512]{2,1,0:T(8,128)S(1)} %get-tuple-element.19.aux_1, ...), custom_call_target="tpu_custom_call", output_to_operand_aliasing={{}: (10, {})} | custom-call | tf_op jit(solution)/shard_map/tangent/pallas_call | solution.py:312
  (14 shorter events, 0.0 us)
Async XLA Ops:
  0.6 4.7 %collective-permute-start = (f32[54,2,128]{2,1,0:T(2,128)}, f32[54,2,128]{2,1,0:T(2,128)S(1)}, u32[]{:S(2)}, u32[]{:S(2)}) collective-permute-start(f32[54,2,128]{2,1,0:T(2,128)} %own.1), channel_id=1, source_target_pairs={{0,1},{1,0},{2,3},{3,2},{4,5},{5,4},{6,7},{7,6},{8,9},{9,8},{10,11... | collective-permute-start | bytes 165896 | tf_op jit(solution)/shard_map/ppermute | solution.py:259
  3.0 4.4 %collective-permute-start.1 = (f32[54,2,128]{2,1,0:T(2,128)}, f32[54,2,128]{2,1,0:T(2,128)S(1)}, u32[]{:S(2)}, u32[]{:S(2)}) collective-permute-start(f32[54,2,128]{2,1,0:T(2,128)} %own.1), channel_id=1, source_target_pairs={{0,63},{1,2},{2,1},{3,4},{4,3},{5,6},{6,5},{7,8},{8,7},{9,10},{10,... | collective-permute-start | bytes 165896 | tf_op jit(solution)/shard_map/ppermute | solution.py:260
  7.3 0.8 %copy-start.3 = (f32[54,2,128]{2,1,0:T(2,128)S(1)}, f32[54,2,128]{2,1,0:T(2,128)}, u32[]{:S(2)}) copy-start(f32[54,2,128]{2,1,0:T(2,128)} %own.1) | copy-start | bytes 165892
  8.2 16.5 %collective-permute-start.3 = (f32[56,512]{1,0:T(8,128)S(1)}, f32[56,512]{1,0:T(8,128)S(1)}, u32[]{:S(2)}, u32[]{:S(2)}) collective-permute-start(f32[56,512]{1,0:T(8,128)S(1)} %near_planes.1.own), channel_id=1, source_target_pairs={{0,128},{128,0},{1,129},{129,1},{2,130},{130,2},{3,131},{131,3},{4... | collective-permute-start | bytes 344072 | tf_op jit(solution)/shard_map/ppermute | solution.py:285
  8.3 1.1 %copy-start = (f32[3,54,2,512]{3,2,1,0:T(2,128)S(1)}, f32[3,54,2,512]{3,2,1,0:T(2,128)}, u32[]{:S(2)}) copy-start(f32[3,54,2,512]{3,2,1,0:T(2,128)} %tangents.1) | copy-start | bytes 1990660
  9.4 0.9 %copy-start.1 = (s32[325,53]{0,1:T(8,128)S(1)}, s32[325,53]{0,1:T(8,128)}, u32[]{:S(2)}) copy-start(s32[325,53]{0,1:T(8,128)} %param.12) | copy-start | bytes 206704
  10.3 0.9 %copy-start.2 = (s32[325,53]{0,1:T(8,128)S(1)}, s32[325,53]{0,1:T(8,128)}, u32[]{:S(2)}) copy-start(s32[325,53]{0,1:T(8,128)} %param.13) | copy-start | bytes 206704
  11.2 0.7 %copy-start.4 = (f32[325]{0:T(512)S(1)}, f32[325]{0:T(512)}, u32[]{:S(2)}) copy-start(f32[325]{0:T(512)} %log_frequency.1) | copy-start | bytes 3904
  11.9 0.7 %copy-start.5 = (f32[325]{0:T(512)S(1)}, f32[325]{0:T(512)}, u32[]{:S(2)}) copy-start(f32[325]{0:T(512)} %energy.1) | copy-start | bytes 3904
  12.6 0.7 %copy-start.6 = (f32[54]{0:T(128)S(1)}, f32[54]{0:T(128)}, u32[]{:S(2)}) copy-start(f32[54]{0:T(128)} %diffusivity.1) | copy-start | bytes 652
  13.2 0.7 %copy-start.7 = (f32[53]{0:T(128)S(1)}, f32[53]{0:T(128)}, u32[]{:S(2)}) copy-start(f32[53]{0:T(128)} %enthalpy.1) | copy-start | bytes 640
  13.9 0.7 %copy-start.8 = (s32[3]{0:T(128)S(1)}, s32[3]{0:T(128)}, u32[]{:S(2)}) copy-start(s32[3]{0:T(128)} %chosen.1) | copy-start | bytes 40
  16.2 17.5 %collective-permute-start.9 = (f32[54,2,512]{2,1,0:T(2,128)S(1)}, f32[54,2,512]{2,1,0:T(2,128)S(1)}, u32[]{:S(2)}, u32[]{:S(2)}) collective-permute-start(f32[54,2,512]{2,1,0:T(2,128)S(1)} %get-tuple-element.23), channel_id=1, source_target_pairs={{0,1},{1,0},{2,3},{3,2},{4,5},{5,4},{6,7},{7,6},{8,9},{9,8},{10,11... | collective-permute-start | bytes 663560 | tf_op jit(solution)/shard_map/ppermute | solution.py:275
  24.7 8.9 %collective-permute-start.2 = (f32[56,512]{1,0:T(8,128)S(1)}, f32[56,512]{1,0:T(8,128)S(1)}, u32[]{:S(2)}, u32[]{:S(2)}) collective-permute-start(f32[56,512]{1,0:T(8,128)S(1)} %near_planes.1.own), channel_id=1, source_target_pairs={{0,64},{64,0},{1,65},{65,1},{2,66},{66,2},{3,67},{67,3},{4,68},{68... | collective-permute-start | bytes 344072 | tf_op jit(solution)/shard_map/ppermute | solution.py:286
  24.7 11.0 %collective-permute-start.4 = (f32[56,512]{1,0:T(8,128)S(1)}, f32[56,512]{1,0:T(8,128)S(1)}, u32[]{:S(2)}, u32[]{:S(2)}) collective-permute-start(f32[56,512]{1,0:T(8,128)S(1)} %collective-permute-done.3.other), channel_id=1, source_target_pairs={{0,64},{64,0},{1,65},{65,1},{2,66},{66,2},{3,67},{67,3},{4,68},{68... | collective-permute-start | bytes 344072 | tf_op jit(solution)/shard_map/ppermute | solution.py:287
  25.2 21.7 %collective-permute-start.10 = (f32[54,2,512]{2,1,0:T(2,128)S(1)}, f32[54,2,512]{2,1,0:T(2,128)S(1)}, u32[]{:S(2)}, u32[]{:S(2)}) collective-permute-start(f32[54,2,512]{2,1,0:T(2,128)S(1)} %get-tuple-element.23), channel_id=1, source_target_pairs={{0,63},{1,2},{2,1},{3,4},{4,3},{5,6},{6,5},{7,8},{8,7},{9,10},{10,... | collective-permute-start | bytes 663560 | tf_op jit(solution)/shard_map/ppermute | solution.py:275
  25.2 27.2 %collective-permute-start.7 = (f32[54,2,512]{2,1,0:T(2,128)S(1)}, f32[54,2,512]{2,1,0:T(2,128)S(1)}, u32[]{:S(2)}, u32[]{:S(2)}) collective-permute-start(f32[54,2,512]{2,1,0:T(2,128)S(1)} %get-tuple-element.22), channel_id=1, source_target_pairs={{0,1},{1,0},{2,3},{3,2},{4,5},{5,4},{6,7},{7,6},{8,9},{9,8},{10,11... | collective-permute-start | bytes 663560 | tf_op jit(solution)/shard_map/ppermute | solution.py:275
  33.6 18.8 %collective-permute-start.8 = (f32[54,2,512]{2,1,0:T(2,128)S(1)}, f32[54,2,512]{2,1,0:T(2,128)S(1)}, u32[]{:S(2)}, u32[]{:S(2)}) collective-permute-start(f32[54,2,512]{2,1,0:T(2,128)S(1)} %get-tuple-element.22), channel_id=1, source_target_pairs={{0,63},{1,2},{2,1},{3,4},{4,3},{5,6},{6,5},{7,8},{8,7},{9,10},{10,... | collective-permute-start | bytes 663560 | tf_op jit(solution)/shard_map/ppermute | solution.py:275
  33.6 24.3 %collective-permute-start.6 = (f32[54,2,512]{2,1,0:T(2,128)S(1)}, f32[54,2,512]{2,1,0:T(2,128)S(1)}, u32[]{:S(2)}, u32[]{:S(2)}) collective-permute-start(f32[54,2,512]{2,1,0:T(2,128)S(1)} %get-tuple-element.17), channel_id=1, source_target_pairs={{0,63},{1,2},{2,1},{3,4},{4,3},{5,6},{6,5},{7,8},{8,7},{9,10},{10,... | collective-permute-start | bytes 663560 | tf_op jit(solution)/shard_map/ppermute | solution.py:275
  35.7 22.3 %collective-permute-start.5 = (f32[54,2,512]{2,1,0:T(2,128)S(1)}, f32[54,2,512]{2,1,0:T(2,128)S(1)}, u32[]{:S(2)}, u32[]{:S(2)}) collective-permute-start(f32[54,2,512]{2,1,0:T(2,128)S(1)} %get-tuple-element.17), channel_id=1, source_target_pairs={{0,1},{1,0},{2,3},{3,2},{4,5},{5,4},{6,7},{7,6},{8,9},{9,8},{10,11... | collective-permute-start | bytes 663560 | tf_op jit(solution)/shard_map/ppermute | solution.py:275

commit v2 on v1

--- a/solution.py
+++ b/solution.py
@@ -1,5 +1,3 @@
-import functools
-
 import jax
 import jax.numpy as jnp
 from jax import lax
@@ -69,10 +67,14 @@
     return total + ref[p - 1, j] + ref[p + 1, j] - 6.0 * c
 
 
-def prepare_kernel(tangents, consumed, made, log_frequency, energy, diffusivity, enthalpy, chosen, t0, t1, t2, w1, w2, spread, sems):
-    copies = [pltpu.make_async_copy(tangents.at[d], t, sems.at[d]) for d, t in enumerate((t0, t1, t2))]
+def prepare_kernel(tangents, consumed_in, made_in, log_frequency_in, energy_in, diffusivity_in, enthalpy_in, chosen, own, w1, w2, spread, *scratch):
+    consumed, made, log_frequency, energy, diffusivity, enthalpy, sems = scratch
+    sources = (consumed_in, made_in, log_frequency_in, energy_in, diffusivity_in, enthalpy_in, tangents)
+    copies = [pltpu.make_async_copy(source, target, sems.at[k]) for k, (source, target) in enumerate(zip(sources, (*scratch[:-1], own)))]
     for copy in copies:
         copy.start()
+    for copy in copies[:-1]:
+        copy.wait()
     lanes = 384
 
     def wide(x):
@@ -108,8 +110,7 @@
     table = jnp.concatenate([table[:48], table[48:64] + placed(rows, (16, lanes))], 0)
     w2[...] = table[:, :RP].astype(bf16)
     spread[...] = jnp.broadcast_to(jnp.pad(diffusivity[...].reshape(1, F), ((0, 0), (0, 128 - F))), (128, 128)).T[:FP]
-    for copy in copies:
-        copy.wait()
+    copies[-1].wait()
 
 
 def sides_of():
@@ -162,7 +163,7 @@
             slope[p + 1, j] = chem[:, p * 128 : (p + 1) * 128]
         return carry
 
-    lax.fori_loop(0, 4, first, 0)
+    lax.fori_loop(0, 4, first, 0, unroll=UNROLL)
 
     def advance(p, j):
         s = slope[p, j] + spread[...] * laplace(state, p, j)
@@ -184,7 +185,7 @@
         slope[3, j] = slope[3, j] + chem[:, 128:]
         return carry
 
-    lax.fori_loop(0, 4, second, 0)
+    lax.fori_loop(0, 4, second, 0, unroll=UNROLL)
     for p, plane in ((2, odd_side), (3, 1 - odd_side)):
         total = slope[p, quarter] + spread[...] * laplace(middle, p, quarter)
         new = state[p, quarter] + 0.1 * total
@@ -198,48 +199,57 @@
     return (production_change - aux_ref[0:FP] * u) * aux_ref[FP : 2 * FP]
 
 
-def tangent_kernel(own, even, odd, rates_1, aux_1, rates_2, aux_2, w1, w2, spread, *rest, d):
-    out, result, state, slope, middle, sem = rest[-6:]
+def tangent_kernel(own, even, odd, rates_1, aux_1, rates_2, aux_2, w1, w2, spread, out, result, state, slope, middle, sems):
     odd_side = sides_of()
     sources = ((odd, odd_side), (odd, 1 - odd_side), (own, odd_side), (own, 1 - odd_side), (even, odd_side), (even, 1 - odd_side))
-    for p, (ref, start) in enumerate(sources):
-        for j in range(4):
-            state[p, j, 48:56, :] = jnp.zeros((8, 128), f32)
-            state[p, j, 0:F, :] = ref[pl.ds(start + 2 * j, F, stride=8), :]
-
-    def first(j, carry):
-        chem = tangent_section(planes_at(state, 1, 4, j), w1[...], w2[...], rates_1.at[j], aux_1.at[j], d)
-        for p in range(4):
-            slope[p + 1, j] = chem[:, p * 128 : (p + 1) * 128]
+    rows = 8 * F
+
+    def written(d):
+        return pltpu.make_async_copy(result.at[d], out.at[pl.ds(d * rows, rows)], sems.at[d])
+
+    def direction(d, carry):
+        for p, (ref, start) in enumerate(sources):
+            for j in range(4):
+                state[p, j, 48:56, :] = jnp.zeros((8, 128), f32)
+                state[p, j, 0:F, :] = ref[pl.ds(d * rows + start + 2 * j, F, stride=8), :]
+
+        def first(j, carry):
+            chem = tangent_section(planes_at(state, 1, 4, j), w1[...], w2[...], rates_1.at[j], aux_1.at[j], d)
+            for p in range(4):
+                slope[p + 1, j] = chem[:, p * 128 : (p + 1) * 128]
+            return carry
+
+        lax.fori_loop(0, 4, first, 0, unroll=UNROLL)
+
+        def diffuse(j, carry):
+            for p in range(1, 5):
+                s = slope[p, j] + spread[...] * laplace(state, p, j)
+                slope[p, j] = s
+                middle[p, j] = state[p, j] + 0.2 * s
+            return carry
+
+        lax.fori_loop(0, 4, diffuse, 0)
+
+        def second(j, carry):
+            chem = tangent_section(planes_at(middle, 2, 3, j), w1[...], w2[...], rates_2.at[j], aux_2.at[j], d)
+            for p, start in ((2, odd_side), (3, 1 - odd_side)):
+                total = slope[p, j] + chem[:, (p - 2) * 128 : (p - 1) * 128] + spread[...] * laplace(middle, p, j)
+                new = state[p, j] + 0.1 * total
+                result[d, pl.ds(start + 2 * j, F, stride=8), :] = new[0:F]
+            return carry
+
+        lax.fori_loop(0, 4, second, 0, unroll=UNROLL)
+        written(d).start()
         return carry
 
-    lax.fori_loop(0, 4, first, 0)
-
-    def diffuse(j, carry):
-        for p in range(1, 5):
-            s = slope[p, j] + spread[...] * laplace(state, p, j)
-            slope[p, j] = s
-            middle[p, j] = state[p, j] + 0.2 * s
-        return carry
-
-    lax.fori_loop(0, 4, diffuse, 0)
-
-    def second(j, carry):
-        chem = tangent_section(planes_at(middle, 2, 3, j), w1[...], w2[...], rates_2.at[j], aux_2.at[j], d)
-        for p, start in ((2, odd_side), (3, 1 - odd_side)):
-            total = slope[p, j] + chem[:, (p - 2) * 128 : (p - 1) * 128] + spread[...] * laplace(middle, p, j)
-            new = state[p, j] + 0.1 * total
-            result[pl.ds(start + 2 * j, F, stride=8), :] = new[0:F]
-        return carry
-
-    lax.fori_loop(0, 4, second, 0)
-    copy = pltpu.make_async_copy(result, out.at[pl.ds(d * 8 * F, 8 * F)], sem)
-    copy.start()
-    copy.wait()
-
-
+    lax.fori_loop(0, 3, direction, 0)
+    for d in range(3):
+        written(d).wait()
+
+
+UNROLL = 2
 VMEM = pl.BlockSpec(memory_space=pltpu.VMEM)
-HBM = pl.BlockSpec(memory_space=pl.ANY)
+HBM = pl.BlockSpec(memory_space=pltpu.HBM)
 
 
 def params(mebibytes):
@@ -256,23 +266,29 @@
     even = [(i, i ^ 1) for i in range(count)]
     odd = [(i, (i + 1 if i & 1 else i - 1) % count) for i in range(count)]
     swap = [(0, 1), (1, 0)]
+    state_odd = lax.ppermute(flame_state, "sp", odd)
+    tangents_odd = lax.ppermute(tangents, "sp", odd)
     state_even = lax.ppermute(flame_state, "sp", even)
-    state_odd = lax.ppermute(flame_state, "sp", odd)
-    *slices, w1, w2, spread = pl.pallas_call(
+    tangents_even = lax.ppermute(tangents, "sp", even)
+    tables = (tangents, reactant_table.T, product_table.T, log_frequency, energy, diffusivity, enthalpy)
+    own, w1, w2, spread = pl.pallas_call(
         prepare_kernel,
         out_shape=(
-            *[jax.ShapeDtypeStruct(tangents.shape[1:], f32)] * 3,
+            jax.ShapeDtypeStruct(tangents.shape, f32),
             jax.ShapeDtypeStruct((RP, 128), bf16),
             jax.ShapeDtypeStruct((64, RP), bf16),
             jax.ShapeDtypeStruct((FP, 128), f32),
         ),
-        in_specs=[HBM, *[VMEM] * 6, pl.BlockSpec(memory_space=pltpu.SMEM)],
-        out_specs=(HBM, HBM, HBM, VMEM, VMEM, VMEM),
-        scratch_shapes=[pltpu.SemaphoreType.DMA((3,))],
+        in_specs=[HBM] * 7 + [pl.BlockSpec(memory_space=pltpu.SMEM)],
+        out_specs=(VMEM,) * 4,
+        scratch_shapes=[
+            *[pltpu.VMEM((F - 1, reactant_table.shape[0]), jnp.int32)] * 2,
+            *[pltpu.VMEM(x.shape, f32) for x in (log_frequency, energy, diffusivity, enthalpy)],
+            pltpu.SemaphoreType.DMA((7,)),
+        ],
         compiler_params=params(4),
         name="prepare",
-    )(tangents, reactant_table.T, product_table.T, log_frequency, energy, diffusivity, enthalpy, direction_index)
-    sides = [(lax.ppermute(t, "sp", even), lax.ppermute(t, "sp", odd)) for t in slices]
+    )(*[pltpu.with_memory_space_constraint(x, pltpu.HBM) for x in tables], direction_index)
 
     near = pl.pallas_call(
         near_kernel,
@@ -304,21 +320,15 @@
         name="nominal",
     )(near, core, other, other_core, state_even, state_odd, w1, w2, spread)
 
-    rows = None
-    for d in range(3):
-        operands = [cell_rows(slices[d]), cell_rows(sides[d][0]), cell_rows(sides[d][1]), rates_1, aux_1, rates_2, aux_2, w1, w2, spread]
-        if d:
-            operands.append(rows)
-        rows = pl.pallas_call(
-            functools.partial(tangent_kernel, d=d),
-            out_shape=jax.ShapeDtypeStruct((3 * 8 * F, 128), f32),
-            in_specs=[VMEM] * 10 + [HBM] * (d > 0),
-            out_specs=HBM,
-            scratch_shapes=[pltpu.VMEM((8 * F, 128), f32), planes, planes, planes, pltpu.SemaphoreType.DMA],
-            input_output_aliases={10: 0} if d else {},
-            compiler_params=params(10),
-            name="tangent",
-        )(*operands)
+    rows = pl.pallas_call(
+        tangent_kernel,
+        out_shape=jax.ShapeDtypeStruct((3 * 8 * F, 128), f32),
+        in_specs=[VMEM] * 10,
+        out_specs=HBM,
+        scratch_shapes=[pltpu.VMEM((3, 8 * F, 128), f32), planes, planes, planes, pltpu.SemaphoreType.DMA((3,))],
+        compiler_params=params(10),
+        name="tangent",
+    )(cell_rows(own), cell_rows(tangents_even), cell_rows(tangents_odd), rates_1, aux_1, rates_2, aux_2, w1, w2, spread)
     rows = rows.reshape(3, F, 4, 2, 128)
     return new_state, jnp.swapaxes(rows, 2, 3).reshape(tangents.shape)
 
@@ -328,4 +338,6 @@
     state = P(None, "sp", GRP)
     sensitivities = P(GRP, None, "sp", None)
     placed = (state, sensitivities, P(GRP), P(), P(), P(), P(), P(), P())
+
+
     return jax.shard_map(shards, mesh=split_mesh, in_specs=placed, out_specs=(state, sensitivities), check_vma=False)

time: 63.8 us -> 54.9 us (0.86)
  the two profiles are of different devices: /device:TPU:2 before, /device:TPU:1 now
where the time goes in v2:
time: 54.9 us; the launch traced here: 54.7 us
  Pallas kernels  18.6 us (34%)
  starting transfers between devices  17.7 us (32%)
  waiting for transfers between devices  16.3 us (30%)
  local copies, waits for them, and re-layouts  1.47 us (3%)
  between operations  0.66 us (1%)
    pallas_call x1, Pallas kernels, shards(): pl.pallas_call(tangent_kernel, out_shape=jax.ShapeDtypeStruct((3 * 8 * F,...  12.2 us
    ppermute x1, waiting for transfers between devices, shards(): state_odd = lax.ppermute(flame_state, 'sp', odd)  10.6 us
    ppermute x1, starting transfers between devices, shards(): tangents_odd = lax.ppermute(tangents, 'sp', odd)  9.74 us
    pallas_call x1, Pallas kernels, shards(): pl.pallas_call(nominal_kernel, out_shape=(jax.ShapeDtypeStruct((4, RP, 51...  4.48 us
    ppermute x1, waiting for transfers between devices, shards(): state_even = lax.ppermute(flame_state, 'sp', even)  4.21 us
    ppermute x1, starting transfers between devices, shards(): other_core = lax.ppermute(other, 'grp_1', swap)  2.68 us
    ppermute x1, starting transfers between devices, shards(): tangents_even = lax.ppermute(tangents, 'sp', even)  2.12 us
    pallas_call x1, Pallas kernels, shards(): pl.pallas_call(prepare_kernel, out_shape=(jax.ShapeDtypeStruct(tangents.s...  1.85 us
  transfers between devices with their start and end apart: 7, of which 3 were waited for; matrix products, arithmetic and copies ran while one was open for 0% of the time, Pallas kernels for 12%

profile of v2, /device:TPU:1, one launch (start us, length us, event | category | flops | bytes accessed | tf_op | source)
XLA Modules:
  0.0 54.7 jit_solution(458786572413185461)
XLA Ops:
  0.6 2.1 %collective-permute-start.5 = (f32[3,54,2,512]{3,2,1,0:T(2,128)}, f32[3,54,2,512]{3,2,1,0:T(2,128)S(1)}, u32[]{:S(2)}, u32[]{:S(2)}) collective-permute-start(f32[3,54,2,512]{3,2,1,0:T(2,128)} %tangents.1), channel_id=1, source_target_pairs={{0,1},{1,0},{2,3},{3,2},{4,5},{5,4},{6,7},{7,6},{8,9},{9,8},{10,11... | collective-permute-start | bytes 1990664 | tf_op jit(solution)/shard_map/ppermute | solution.py:272
  2.7 9.7 %collective-permute-start.6 = (f32[3,54,2,512]{3,2,1,0:T(2,128)}, f32[3,54,2,512]{3,2,1,0:T(2,128)S(1)}, u32[]{:S(2)}, u32[]{:S(2)}) collective-permute-start(f32[3,54,2,512]{3,2,1,0:T(2,128)} %tangents.1), channel_id=1, source_target_pairs={{0,63},{1,2},{2,1},{3,4},{4,3},{5,6},{6,5},{7,8},{8,7},{9,10},{10,... | collective-permute-start | bytes 1990664 | tf_op jit(solution)/shard_map/ppermute | solution.py:270
  12.5 0.0 collective-permute-start
  12.5 0.9 %collective-permute-start.1 = (f32[54,2,128]{2,1,0:T(2,128)}, f32[54,2,128]{2,1,0:T(2,128)S(1)}, u32[]{:S(2)}, u32[]{:S(2)}) collective-permute-start(f32[54,2,128]{2,1,0:T(2,128)} %own.1), channel_id=1, source_target_pairs={{0,63},{1,2},{2,1},{3,4},{4,3},{5,6},{6,5},{7,8},{8,7},{9,10},{10,... | collective-permute-start | bytes 165896 | tf_op jit(solution)/shard_map/ppermute | solution.py:269
  13.4 4.2 %collective-permute-done.even = f32[54,2,128]{2,1,0:T(2,128)S(1)} collective-permute-done((f32[54,2,128]{2,1,0:T(2,128)}, f32[54,2,128]{2,1,0:T(2,128)S(1)}, u32[]{:S(2)}, u32[]{:S(2)}) %collective-permute-start) | collective-permute-done | bytes 55328 | tf_op jit(solution)/shard_map/ppermute | solution.py:271
  17.6 10.6 %collective-permute-done.1.odd = f32[54,2,128]{2,1,0:T(2,128)S(1)} collective-permute-done((f32[54,2,128]{2,1,0:T(2,128)}, f32[54,2,128]{2,1,0:T(2,128)S(1)}, u32[]{:S(2)}, u32[]{:S(2)}) %collective-permute-start.1) | collective-permute-done | bytes 55328 | tf_op jit(solution)/shard_map/ppermute | solution.py:269
  28.2 0.0 copy-start
  28.2 0.8 %copy-done = f32[54,2,128]{2,1,0:T(2,128)S(1)} copy-done((f32[54,2,128]{2,1,0:T(2,128)S(1)}, f32[54,2,128]{2,1,0:T(2,128)}, u32[]{:S(2)}) %copy-start) | copy-done | bytes 55320
  29.1 0.1 near_planes.1.own
  29.1 0.5 collective-permute-start.3
  29.6 1.8 %collective-permute-start.2 = (f32[56,512]{1,0:T(8,128)S(1)}, f32[56,512]{1,0:T(8,128)S(1)}, u32[]{:S(2)}, u32[]{:S(2)}) collective-permute-start(f32[56,512]{1,0:T(8,128)S(1)} %near_planes.1.own), channel_id=1, source_target_pairs={{0,64},{64,0},{1,65},{65,1},{2,66},{66,2},{3,67},{67,3},{4,68},{68... | collective-permute-start | bytes 344072 | tf_op jit(solution)/shard_map/ppermute | solution.py:302
  31.4 1.4 %collective-permute-done.3.other = f32[56,512]{1,0:T(8,128)S(1)} collective-permute-done((f32[56,512]{1,0:T(8,128)S(1)}, f32[56,512]{1,0:T(8,128)S(1)}, u32[]{:S(2)}, u32[]{:S(2)}) %collective-permute-start.3) | collective-permute-done | bytes 114720 | tf_op jit(solution)/shard_map/ppermute | solution.py:301
  32.9 2.7 %collective-permute-start.4 = (f32[56,512]{1,0:T(8,128)S(1)}, f32[56,512]{1,0:T(8,128)S(1)}, u32[]{:S(2)}, u32[]{:S(2)}) collective-permute-start(f32[56,512]{1,0:T(8,128)S(1)} %collective-permute-done.3.other), channel_id=1, source_target_pairs={{0,64},{64,0},{1,65},{65,1},{2,66},{66,2},{3,67},{67,3},{4,68},{68... | collective-permute-start | bytes 344072 | tf_op jit(solution)/shard_map/ppermute | solution.py:303
  35.5 0.0 copy-start.1
  35.5 0.7 %copy-done.1 = s32[3]{0:T(128)S(1)} copy-done((s32[3]{0:T(128)S(1)}, s32[3]{0:T(128)}, u32[]{:S(2)}) %copy-start.1) | copy-done | bytes 36
  36.2 1.8 %prepare.1 = (f32[3,54,2,512]{3,2,1,0:T(2,128)S(1)}, bf16[336,128]{1,0:T(8,128)(2,1)S(1)}, bf16[64,336]{1,0:T(8,128)(2,1)S(1)}, f32[56,128]{1,0:T(8,128)S(1)}) custom-call(f32[3,54,2,512]{3,2,1,0:T(2,128)} %tangents.1, s32[53,325]{1,0:T(8,128)} %bitcast.26, s32[53,325]{1,0:T(8,128)} %bitcast.27, f32[325]{0:T(512)} %log_frequency_in.1, f32[325]{0:T(512)} %energy_in.1, ...), custom_call_target="tpu_custom_call" | custom-call | tf_op jit(solution)/shard_map/prepare/pallas_call | solution.py:274
  38.0 0.0 collective-permute-done.2.core
  38.1 0.0 collective-permute-done.4.other_core
  38.1 4.5 %nominal.1 = (f32[4,336,512]{2,1,0:T(8,128)S(1)}, f32[4,120,512]{2,1,0:T(8,128)S(1)}, f32[4,336,256]{2,1,0:T(8,128)S(1)}, f32[4,120,256]{2,1,0:T(8,128)S(1)}, f32[54,2,128]{2,1,0:T(2,128)}) custom-call(f32[56,512]{1,0:T(8,128)S(1)} %near_planes.1.own, f32[56,512]{1,0:T(8,128)S(1)} %collective-permute-done.2.core, ...), custom_call_target="tpu_custom_call" | custom-call | tf_op jit(solution)/shard_map/nominal/pallas_call | solution.py:307
  42.6 0.0 collective-permute-done.5
  42.6 0.0 collective-permute-done.6
  42.6 12.2 %tangent.1 = f32[1296,128]{1,0:T(8,128)} custom-call(f32[1296,128]{1,0:T(8,128)S(1)} %bitcast.24, f32[1296,128]{1,0:T(8,128)S(1)} %bitcast.22, f32[1296,128]{1,0:T(8,128)S(1)} %bitcast.23, f32[4,336,512]{2,1,0:T(8,128)S(1)} %get-tuple-element.16.rates_1, f32[4,120,512]{2,1,0:T(8,128)S(1)} %get-tuple-element.17.aux_1, ...), custom_call_target="tpu_custom_call" | custom-call | tf_op jit(solution)/shard_map/tangent/pallas_call | solution.py:323
Async XLA Ops:
  0.6 41.9 %collective-permute-start.5 = (f32[3,54,2,512]{3,2,1,0:T(2,128)}, f32[3,54,2,512]{3,2,1,0:T(2,128)S(1)}, u32[]{:S(2)}, u32[]{:S(2)}) collective-permute-start(f32[3,54,2,512]{3,2,1,0:T(2,128)} %tangents.1), channel_id=1, source_target_pairs={{0,1},{1,0},{2,3},{3,2},{4,5},{5,4},{6,7},{7,6},{8,9},{9,8},{10,11... | collective-permute-start | bytes 1990664 | tf_op jit(solution)/shard_map/ppermute | solution.py:272
  2.7 39.8 %collective-permute-start.6 = (f32[3,54,2,512]{3,2,1,0:T(2,128)}, f32[3,54,2,512]{3,2,1,0:T(2,128)S(1)}, u32[]{:S(2)}, u32[]{:S(2)}) collective-permute-start(f32[3,54,2,512]{3,2,1,0:T(2,128)} %tangents.1), channel_id=1, source_target_pairs={{0,63},{1,2},{2,1},{3,4},{4,3},{5,6},{6,5},{7,8},{8,7},{9,10},{10,... | collective-permute-start | bytes 1990664 | tf_op jit(solution)/shard_map/ppermute | solution.py:270
  12.5 5.1 %collective-permute-start = (f32[54,2,128]{2,1,0:T(2,128)}, f32[54,2,128]{2,1,0:T(2,128)S(1)}, u32[]{:S(2)}, u32[]{:S(2)}) collective-permute-start(f32[54,2,128]{2,1,0:T(2,128)} %own.1), channel_id=1, source_target_pairs={{0,1},{1,0},{2,3},{3,2},{4,5},{5,4},{6,7},{7,6},{8,9},{9,8},{10,11... | collective-permute-start | bytes 165896 | tf_op jit(solution)/shard_map/ppermute | solution.py:271
  12.5 15.8 %collective-permute-start.1 = (f32[54,2,128]{2,1,0:T(2,128)}, f32[54,2,128]{2,1,0:T(2,128)S(1)}, u32[]{:S(2)}, u32[]{:S(2)}) collective-permute-start(f32[54,2,128]{2,1,0:T(2,128)} %own.1), channel_id=1, source_target_pairs={{0,63},{1,2},{2,1},{3,4},{4,3},{5,6},{6,5},{7,8},{8,7},{9,10},{10,... | collective-permute-start | bytes 165896 | tf_op jit(solution)/shard_map/ppermute | solution.py:269
  28.2 0.8 %copy-start = (f32[54,2,128]{2,1,0:T(2,128)S(1)}, f32[54,2,128]{2,1,0:T(2,128)}, u32[]{:S(2)}) copy-start(f32[54,2,128]{2,1,0:T(2,128)} %own.1) | copy-start | bytes 165892
  29.1 3.7 %collective-permute-start.3 = (f32[56,512]{1,0:T(8,128)S(1)}, f32[56,512]{1,0:T(8,128)S(1)}, u32[]{:S(2)}, u32[]{:S(2)}) collective-permute-start(f32[56,512]{1,0:T(8,128)S(1)} %near_planes.1.own), channel_id=1, source_target_pairs={{0,128},{128,0},{1,129},{129,1},{2,130},{130,2},{3,131},{131,3},{4... | collective-permute-start | bytes 344072 | tf_op jit(solution)/shard_map/ppermute | solution.py:301
  29.6 8.4 %collective-permute-start.2 = (f32[56,512]{1,0:T(8,128)S(1)}, f32[56,512]{1,0:T(8,128)S(1)}, u32[]{:S(2)}, u32[]{:S(2)}) collective-permute-start(f32[56,512]{1,0:T(8,128)S(1)} %near_planes.1.own), channel_id=1, source_target_pairs={{0,64},{64,0},{1,65},{65,1},{2,66},{66,2},{3,67},{67,3},{4,68},{68... | collective-permute-start | bytes 344072 | tf_op jit(solution)/shard_map/ppermute | solution.py:302
  32.9 5.2 %collective-permute-start.4 = (f32[56,512]{1,0:T(8,128)S(1)}, f32[56,512]{1,0:T(8,128)S(1)}, u32[]{:S(2)}, u32[]{:S(2)}) collective-permute-start(f32[56,512]{1,0:T(8,128)S(1)} %collective-permute-done.3.other), channel_id=1, source_target_pairs={{0,64},{64,0},{1,65},{65,1},{2,66},{66,2},{3,67},{67,3},{4,68},{68... | collective-permute-start | bytes 344072 | tf_op jit(solution)/shard_map/ppermute | solution.py:303
  35.5 0.7 %copy-start.1 = (s32[3]{0:T(128)S(1)}, s32[3]{0:T(128)}, u32[]{:S(2)}) copy-start(s32[3]{0:T(128)} %chosen.1) | copy-start | bytes 40
